TPU v7x, 8 devices: a whole 2x2x1 slice. The times are simulated.
8 devices in a mesh: dp: 1 (over z), tp: 2 (over y), sp: 4 (over x, core).
Axes of the slice: x: 2, y: 2, z: 1, core: 2. Of those that a mesh axis runs over, the one named last changes fastest.
Arguments:
- hidden: bfloat16 [64, 3072], P('dp')
- norm_scale: bfloat16 [3072], replicated
- w_qkv: bfloat16 [3072, 5120], P(None, 'tp')
- w_out: bfloat16 [3072, 3072], P('tp')
- k_cache: bfloat16 [64, 1024, 8, 128], P('dp', 'sp', 'tp')
- v_cache: bfloat16 [64, 1024, 8, 128], P('dp', 'sp', 'tp')
- positions: int32 [64], P('dp')
Outputs:
- output 1: bfloat16 [64, 3072], P('dp')
- output 2: bfloat16 [64, 1024, 8, 128], P('dp', 'sp', 'tp')
- output 3: bfloat16 [64, 1024, 8, 128], P('dp', 'sp', 'tp')
All inputs are finite; a program needn't handle non-finite values.
Results may differ from a plain program's by a relative error of at most 0.00645291.
Values sent between devices are 32-bit elements.
A program may use at most 1 GiB of HBM per device.

v0:
```python
import math
import jax
import jax.numpy as jnp
from jax import lax
from jax.sharding import PartitionSpec as P


def rope_apply(head_vals, positions):
    half_dim = head_vals.shape[-1] // 2
    inv_freq = jnp.exp(jnp.arange(half_dim, dtype=jnp.float32) * (-2.0 * math.log(500000.0) / head_vals.shape[-1]))
    angles = positions.astype(jnp.float32)[:, None] * inv_freq[None, :]
    cos_part = jnp.cos(angles)[:, None, None, :]
    sin_part = jnp.sin(angles)[:, None, None, :]
    first_half = head_vals[..., :half_dim]
    second_half = head_vals[..., half_dim:]
    return jnp.concatenate([first_half * cos_part - second_half * sin_part, second_half * cos_part + first_half * sin_part], axis=-1)


def layer_norm_bf16(hidden_f32, norm_scale):
    row_mean = jnp.mean(hidden_f32, axis=-1, keepdims=True)
    centered = hidden_f32 - row_mean
    row_var = jnp.mean(centered * centered, axis=-1, keepdims=True)
    return (centered * lax.rsqrt(row_var + 1e-5) * norm_scale.astype(jnp.float32)).astype(jnp.bfloat16)


def solution(mesh):
    cache_spec = P('dp', 'sp', 'tp', None)

    def local_step(hidden, norm_scale, w_qkv, w_out, k_cache, v_cache, positions):
        n_seq, seq_local, kv_local, head_dim = k_cache.shape
        q_per_kv = w_qkv.shape[1] // (kv_local * head_dim) - 2
        hidden_f32 = hidden.astype(jnp.float32)
        normed = layer_norm_bf16(hidden_f32, norm_scale)
        qkv_proj = jnp.clip(jnp.dot(normed, w_qkv, preferred_element_type=jnp.float32).astype(jnp.bfloat16), -8.0, 8.0)
        grouped = qkv_proj.reshape(n_seq, kv_local, q_per_kv + 2, head_dim)
        rotated = rope_apply(grouped[:, :, : q_per_kv + 1].astype(jnp.float32), positions).astype(jnp.bfloat16)
        queries = rotated[:, :, :q_per_kv]
        row_index = lax.axis_index('sp') * seq_local + jnp.arange(seq_local)
        new_row = (row_index[None, :] == positions[:, None])[:, :, None, None]
        k_upd = jnp.where(new_row, rotated[:, :, q_per_kv][:, None], k_cache)
        v_upd = jnp.where(new_row, grouped[:, :, q_per_kv + 1][:, None], v_cache)
        scores = jnp.einsum('bgqd,bsgd->bgqs', queries, k_upd, preferred_element_type=jnp.float32) * (head_dim ** -0.5)
        valid_mask = row_index[None, :] <= positions[:, None]
        scores = jnp.where(valid_mask[:, None, None, :], scores, -1e30)
        local_max = jnp.max(scores, axis=-1)
        weights = jnp.exp(scores - local_max[..., None])
        local_sum = jnp.sum(weights, axis=-1)
        local_out = jnp.einsum('bgqs,bsgd->bgqd', weights.astype(jnp.bfloat16), v_upd, preferred_element_type=jnp.float32)
        global_max = lax.pmax(local_max, 'sp')
        factor = jnp.exp(local_max - global_max)
        packed = jnp.concatenate([local_out * factor[..., None], (local_sum * factor)[..., None]], axis=-1)
        merged = lax.psum(packed, 'sp')
        attn_out = merged[..., :head_dim] / merged[..., head_dim:]
        attn_flat = attn_out.reshape(n_seq, kv_local * q_per_kv * head_dim).astype(jnp.bfloat16)
        head_part = jnp.dot(attn_flat, w_out, preferred_element_type=jnp.float32)
        proj_sum = lax.psum(head_part, 'tp')
        h_out = (hidden_f32 + proj_sum).astype(jnp.bfloat16)
        return h_out, k_upd, v_upd

    return jax.shard_map(
        local_step,
        mesh=mesh,
        in_specs=(P('dp', None), P(None), P(None, 'tp'), P('tp', None), cache_spec, cache_spec, P('dp')),
        out_specs=(P('dp', None), cache_spec, cache_spec),
        check_vma=False,
    )
```

profile of v0, /device:TPU:0, one launch (start us, length us, event | category | flops | bytes accessed | tf_op | source)
XLA Modules:
  0.0 163.9 jit_solution(9718936736886576401)
XLA Ops:
  7.2 0.0 copy-start.1
  7.2 0.0 all-reduce.3.cloned.1.call-start
  7.2 1.1 convert_reduce_fusion
  8.4 1.3 fusion.18
  9.7 0.7 convert_element_type.36
  10.4 8.5 %fusion.4 = bf16[64,2560]{1,0:T(8,128)(2,1)S(1)} fusion(bf16[3072,2560]{1,0:T(8,128)(2,1)} %param.9, bf16[64,3072]{1,0:T(8,128)(2,1)} %param.7, f32[3072]{0:T(1024)S(1)} %convert_element_type.36, f32[64]{0:T(128)S(1)} %add_rsqrt_fusion, f32[64]{0:T(128)S(1)} %broadcast_multiply_fusion), kind=kOutput, calls=%fused_computation.7 | convolution fusion | flops 1007943680 | bytes 16462336 | tf_op jit(solution)/shard_map/dot_general | solution.py:34
  18.9 0.4 reshape.131
  19.3 0.1 slice.37
  19.5 0.1 slice_convert_fusion
  19.6 0.0 copy-done.1
  19.6 0.1 broadcast_compare_fusion.1
  19.7 0.1 copy.27
  19.8 0.2 multiply_cosine_fusion
  20.0 0.5 subtract_convert_fusion
  20.5 0.5 pad_maximum_fusion.1
  21.0 0.1 copy.24
  21.1 25.9 %broadcast_select_fusion = (bf16[64,256,4,128]{3,2,1,0:T(4,128)(2,1)}, bf16[64,256,4,128]{3,2,1,0:T(4,128)(2,1)}) fusion(bf16[64,256,4,128]{3,2,1,0:T(4,128)(2,1)} %param.12, pred[64,256]{1,0:T(8,128)(4,1)S(1)} %get-tuple-element.10, bf16[64,4,128]{2,1,0:T(4,128)(2,1)S(1)} %copy.27, bf16[64,256,4,128]{3,2,1,0:T(4,128)(2,1)} %param.11, ...), kind=kLoop, calls=%fused_computation.4 | loop fusion | flops 16777216 | bytes 67256320 | tf_op jit(solution)/shard_map/jit(_where)/select_n | solution.py:41
  47.0 10.4 %fusion.35 = (f32[64,4,3]{2,1,0:T(4,128)S(1)}, f32[64,4,3,256]{3,2,1,0:T(4,128)S(1)}) fusion(bf16[64,256,4,128]{3,2,1,0:T(4,128)(2,1)} %get-tuple-element.8, bf16[64,4,4,64]{3,2,1,0:T(4,128)(2,1)S(1)} %get-tuple-element.6, bf16[64,4,4,64]{3,2,1,0:T(4,128)(2,1)S(1)} %get-tuple-element.5, pred[64,256]{1,0:T(8,128)(4,1)S(1)} %get-tuple-element.9), kind=kOutput, calls=%fused_computation.52 | convolution fusion | flops 51313920 | bytes 17845248 | tf_op jit(solution)/shard_map/bgqd,bsgd->bgqs/dot_general | solution.py:42
  57.4 15.0 %pmax.7 = f32[64,4,3]{2,1,0:T(4,128)S(1)} all-reduce(f32[64,4,3]{2,1,0:T(4,128)S(1)} %get-tuple-element.13), channel_id=1, replica_groups=mesh['dp'=1,'tp'=2,'sp'=4] {'sp'}, use_global_device_ids=true, to_apply=%region_3.4 | all-reduce | flops 768 | bytes 6144 | tf_op jit(solution)/shard_map/pmax | solution.py:49
  72.4 0.8 fusion.16
  73.2 0.1 multiply_bitcast_fusion
  73.3 1.7 %copy.30 = f32[64,4,3,1]{3,2,1,0:T(4,128)S(1)} copy(f32[64,4,3,1]{2,1,0,3:T(4,128)S(1)} %get-tuple-element.3) | data formatting | bytes 6144 | tf_op jit(solution)/shard_map/broadcast_in_dim | solution.py:51
  75.0 8.1 %fusion.8 = f32[64,4,3,128]{3,2,1,0:T(4,128)S(1)} fusion(bf16[64,256,4,128]{3,2,1,0:T(4,128)(2,1)} %get-tuple-element.7, f32[64,4,3,256]{3,2,1,0:T(4,128)S(1)} %get-tuple-element.14, f32[64,4,3]{2,1,0:T(4,128)S(1)} %get-tuple-element.13, f32[64,4,3]{2,1,0:T(4,128)S(1)} %get-tuple-element.4), kind=kOutput, calls=%fused_computation.9 | convolution fusion | flops 50823168 | bytes 17963008 | tf_op jit(solution)/shard_map/bgqs,bsgd->bgqd/dot_general | solution.py:48
  83.0 0.0 copy-start
  83.0 1.3 pad_maximum_fusion
  84.3 0.0 all-reduce.3.cloned.1.call-update
  84.4 0.0 all-reduce.5.cloned.1.call-start
  84.4 31.0 %all-reduce.3.cloned.1.call-done = f32[64,4,3,129]{3,2,1,0:T(4,128)} async-done(((f32[64,4,3,129]{3,2,1,0:T(4,128)}), f32[64,4,3,129]{3,2,1,0:T(4,128)}) %all-reduce.3.cloned.1.call-update) | async-done | bytes 396304 | tf_op jit(solution)/shard_map/psum | solution.py:52
  115.4 1.1 slice.39
  116.5 1.6 copy.35
  118.2 1.4 fusion.24
  119.6 0.2 convert_element_type.43
  119.7 6.3 %fusion.36 = f32[64,3072]{1,0:T(8,128)} fusion(bf16[64,1536]{1,0:T(8,128)(2,1)S(1)} %convert_element_type.43, bf16[1536,3072]{1,0:T(8,128)(2,1)} %param.10), kind=kOutput, calls=%fused_computation.53 | convolution fusion | flops 603979776 | bytes 10420224 | tf_op jit(solution)/shard_map/dot_general | solution.py:55
  126.1 0.0 all-reduce.5.cloned.1.call-update
  126.1 29.0 %all-reduce.5.cloned.1.call-done = f32[64,3072]{1,0:T(8,128)} async-done(((f32[64,3072]{1,0:T(8,128)}), f32[64,3072]{1,0:T(8,128)}) %all-reduce.5.cloned.1.call-update) | async-done | bytes 786448 | tf_op jit(solution)/shard_map/psum | solution.py:56
  155.1 0.0 copy-done
  155.1 1.9 %fusion.21 = bf16[64,3072]{1,0:T(8,128)(2,1)} fusion(f32[64,3072]{1,0:T(8,128)} %all-reduce.5.cloned.1.call-done, bf16[64,3072]{1,0:T(8,128)(2,1)S(1)} %copy-done), kind=kLoop, calls=%fused_computation.23 | loop fusion | flops 589824 | bytes 1572864 | tf_op jit(solution)/shard_map/convert_element_type | solution.py:57
  (7 shorter events, 0.1 us)
Async XLA Ops:
  7.2 12.4 %copy-start.1 = (s32[64]{0:T(128)S(1)}, s32[64]{0:T(128)}, u32[]{:S(2)}) copy-start(s32[64]{0:T(128)} %param.13) | copy-start | bytes 772
  7.2 108.2 %all-reduce.3.cloned.1.call-start = ((), (), s32[]{:S(2)}) async-start(), calls=%async_computation | async-start | bytes 2097152 | tf_op jit(solution)/shard_map/psum | solution.py:52
  83.0 72.1 %copy-start = (bf16[64,3072]{1,0:T(8,128)(2,1)S(1)}, bf16[64,3072]{1,0:T(8,128)(2,1)}, u32[]{:S(2)}) copy-start(bf16[64,3072]{1,0:T(8,128)(2,1)} %param.7) | copy-start | bytes 1179652
  84.4 70.7 %all-reduce.5.cloned.1.call-start = ((), (), s32[]{:S(2)}) async-start(), calls=%async_computation.1 | async-start | bytes 1572864 | tf_op jit(solution)/shard_map/psum | solution.py:56
Sparse Core Ops, SparseCore 0:
  84.5 30.8 all-reduce.2
  126.2 28.8 all-reduce.4
where the time goes:
time: 164 us
  waiting for transfers between devices  60 us (37%)
  other arithmetic  35.9 us (22%)
  matrix products  33.3 us (20%)
  blocking collectives  15 us (9%)
  between operations  14.2 us (9%)
  local copies, waits for them, and re-layouts  5.28 us (3%)
    psum x1, waiting for transfers between devices, local_step(): merged = lax.psum(packed, 'sp')  31 us
    psum x1, waiting for transfers between devices, local_step(): proj_sum = lax.psum(head_part, 'tp')  29 us
    select_n x1, other arithmetic, local_step(): v_upd = jnp.where(new_row, grouped[:, :, q_per_kv + 1][:, None], v_cache)  25.9 us
    pmax x1, blocking collectives, local_step(): global_max = lax.pmax(local_max, 'sp')  15 us
    dot_general x1, matrix products, local_step(): jnp.einsum('bgqd,bsgd->bgqs', queries, k_upd, preferred_element_type=jnp....  10.4 us
    dot_general x1, matrix products, local_step(): jnp.dot(normed, w_qkv, preferred_element_type=jnp.float32)  8.53 us
    dot_general x1, matrix products, local_step(): jnp.einsum('bgqs,bsgd->bgqd', weights.astype(jnp.bfloat16), v_upd, prefer...  8.06 us
    dot_general x1, matrix products, local_step(): head_part = jnp.dot(attn_flat, w_out, preferred_element_type=jnp.float32)  6.34 us
  transfers between devices with their start and end apart: 2, of which 2 were waited for; matrix products, arithmetic and copies ran while one was open for 0% of the time, Pallas kernels for 0%

commit v1 on v0

v1 whole, which is shorter than its diff:
```python
import math
import jax
import jax.numpy as jnp
import numpy as np
from jax import lax
from jax.experimental import pallas as pl
from jax.experimental.pallas import tpu as pltpu
from jax.sharding import PartitionSpec as P

MESH = pl.DeviceIdType.MESH
NEG = -1e30
MIB = 1024 * 1024
N_SP = 4
GROUP = 8
W_CHUNKS = 6
W_SLOTS = 3
HELD = 7
JOB = 2
SLOTS = 4
W_VMEM = 3


def attend_kernel(dims, pos, hidden, norm_scale, cos2, sin2, w_qkv, w_out, k_in, v_in,
                  h_out, k_vm, v_vm, new_k, new_v,
                  u, wq, acc, wo, k_rest, v_rest, q_rows, kn_rows, vn_rows, tok, part, recv, merged, proj, proj_in, sums,
                  w_sem, wo_sem, k_sem, v_sem, part_send, part_recv, proj_send, proj_recv, sum_send, sum_recv):
    n_seq, rows, kv, head, per_kv, d_model = dims
    n_heads = kv * per_kv
    n_groups = n_seq // GROUP
    pair_rows = 2 * n_heads
    own = n_seq // N_SP
    w_rows = d_model // W_CHUNKS
    sp = lax.axis_index('sp')
    tp = lax.axis_index('tp')
    seq_local = rows // kv
    scale2 = head ** -0.5 * math.log2(math.e)

    def w_copy(c):
        return pltpu.make_async_copy(w_qkv.at[pl.ds(c * w_rows, w_rows)], wq.at[c % W_SLOTS], w_sem.at[c])

    def held(ref, rest, n_held, g):
        return (ref, g) if g < n_held else (rest, g - n_held)

    def cache_copy(src, ref, rest, n_held, sem, g):
        dst, i = held(ref, rest, n_held, g)
        return pltpu.make_async_copy(src.at[pl.ds(g * GROUP, GROUP)], dst.at[pl.ds(i * GROUP, GROUP)], sem.at[g])

    def k_copy(g):
        return cache_copy(k_in, k_vm, k_rest, HELD, k_sem, g)

    def v_copy(g):
        return cache_copy(v_in, v_vm, v_rest, HELD, v_sem, g)

    wo_copy = pltpu.make_async_copy(w_out, wo, wo_sem)
    for c in range(W_SLOTS):
        w_copy(c).start()
    for g in range(n_groups - W_CHUNKS):
        k_copy(g).start()
        v_copy(g).start()

    barrier = pltpu.get_barrier_semaphore()
    for s in range(1, N_SP):
        pl.semaphore_signal(barrier, inc=1, device_id={'sp': lax.rem(sp + s, N_SP)}, device_id_type=MESH)
    pl.semaphore_signal(barrier, inc=1, device_id={'tp': 1 - tp}, device_id_type=MESH)

    hid = hidden[...].astype(jnp.float32)
    mean = jnp.mean(hid, axis=-1, keepdims=True)
    cen = hid - mean
    var = jnp.mean(cen * cen, axis=-1, keepdims=True)
    normed = (cen * lax.rsqrt(var + 1e-5) * norm_scale[...].astype(jnp.float32)).astype(jnp.bfloat16)
    for c in range(W_CHUNKS):
        u[c] = normed[:, c * w_rows:(c + 1) * w_rows]

    col = lax.broadcasted_iota(jnp.int32, (pair_rows, rows), 1)
    row = lax.broadcasted_iota(jnp.int32, (pair_rows, rows), 0)
    row_kv = lax.rem(row, n_heads) // per_kv
    tok[...] = jnp.where(lax.rem(col, kv) == row_kv, sp * seq_local + col // kv, 1 << 30)

    acc[...] = jnp.zeros_like(acc)

    for c in range(W_CHUNKS):
        w_copy(c).wait()
        g = c + (n_groups - W_CHUNKS)
        k_copy(g).start()
        v_copy(g).start()
        acc[...] += jnp.dot(u[c], wq[c % W_SLOTS], preferred_element_type=jnp.float32)
        if c + W_SLOTS < W_CHUNKS:
            w_copy(c + W_SLOTS).start()

    wo_copy.start()

    c2 = cos2[...]
    s2 = sin2[...]
    for g in range(kv):
        for j in range(per_kv + 2):
            lo = (g * (per_kv + 2) + j) * head
            x = jnp.clip(acc[:, lo:lo + head].astype(jnp.bfloat16).astype(jnp.float32), -8.0, 8.0)
            if j <= per_kv:
                x = (x * c2 + pltpu.roll(x, head // 2, 1) * s2).astype(jnp.bfloat16).astype(jnp.float32)
            if j < per_kv:
                q_rows[pl.ds(g * per_kv + j, n_seq, stride=n_heads), :] = x
            else:
                wide, rep = (kn_rows, new_k) if j == per_kv else (vn_rows, new_v)
                for i in range(per_kv):
                    wide[pl.ds(g * per_kv + i, n_seq, stride=n_heads), :] = x
                for i in range(16 // kv):
                    rep[pl.ds(i * kv + g, n_seq, stride=16), :] = x

    pl.semaphore_wait(barrier, N_SP)

    prow = lax.broadcasted_iota(jnp.int32, (pair_rows, 1), 0)
    first = prow < n_heads

    def part_copy(g, s):
        dst = lax.rem(sp + s, N_SP)
        return pltpu.make_async_remote_copy(
            src_ref=part.at[g, dst], dst_ref=recv.at[g, s - 1],
            send_sem=part_send.at[g, s - 1], recv_sem=part_recv.at[g, s - 1],
            device_id={'sp': dst}, device_id_type=MESH)

    def group_step(g, k_ref, v_ref, k_off, v_off):
        for d in range(N_SP):
            b = g * GROUP + 2 * d
            kb, vb = b - k_off, b - v_off
            q = q_rows[pl.ds(pl.multiple_of((g * N_SP + d) * pair_rows, 8), pair_rows), :]
            zero = jnp.zeros_like(q)
            q_blk = jnp.concatenate([jnp.where(first, q, zero), jnp.where(first, zero, q)], axis=1).astype(jnp.bfloat16)
            k_cat = jnp.concatenate([k_ref[kb], k_ref[kb + 1]], axis=1)
            s = lax.dot_general(q_blk, k_cat, (((1,), (1,)), ((), ())), preferred_element_type=jnp.float32)
            limit = jnp.where(first, pos[b], pos[b + 1])
            s = jnp.where(tok[...] < limit, s, NEG)
            m = jnp.max(s, axis=-1, keepdims=True)
            w = jnp.exp2((s - m) * scale2)
            l = jnp.sum(w, axis=-1, keepdims=True)
            v_cat = jnp.concatenate([v_ref[vb], v_ref[vb + 1]], axis=1)
            o = jnp.dot(w.astype(jnp.bfloat16), v_cat, preferred_element_type=jnp.float32)
            part[g, d, :, :head] = jnp.where(first, o[:, :head], o[:, head:])
            lane = lax.broadcasted_iota(jnp.int32, (pair_rows, head), 1)
            part[g, d, :, head:] = jnp.where(lane < head // 2, m, l)
        for s in range(1, N_SP):
            part_copy(g, s).start()

    def held_step(g, carry):
        s = pl.ds(g * GROUP, GROUP)
        pltpu.make_async_copy(k_in.at[s], k_vm.at[s], k_sem.at[g]).wait()
        pltpu.make_async_copy(v_in.at[s], v_vm.at[s], v_sem.at[g]).wait()
        group_step(g, k_vm, v_vm, 0, 0)
        return carry

    lax.fori_loop(0, HELD, held_step, 0)
    for g in range(HELD, n_groups):
        k_copy(g).wait()
        v_copy(g).wait()
        k_ref, ki = held(k_vm, k_rest, HELD, g)
        v_ref, vi = held(v_vm, v_rest, HELD, g)
        group_step(g, k_ref, v_ref, (g - ki) * GROUP, (g - vi) * GROUP)

    def merge_step(g, carry):
        for s in range(1, N_SP):
            part_copy(g, s).wait()
        r = pl.ds(pl.multiple_of((g * N_SP + sp) * pair_rows, 8), pair_rows)
        s_new = jnp.sum(q_rows[r, :] * kn_rows[r, :], axis=-1, keepdims=True)
        outs = [part[g, sp]] + [recv[g, s] for s in range(N_SP - 1)]
        ms = [x[:, head:head + 1] for x in outs]
        ls = [x[:, head + head // 2:head + head // 2 + 1] for x in outs]
        top = s_new
        for m in ms:
            top = jnp.maximum(top, m)
        f = jnp.exp2((s_new - top) * scale2)
        o = f * vn_rows[r, :]
        l = f
        for x, m, ll in zip(outs, ms, ls):
            f = jnp.exp2((m - top) * scale2)
            o = o + f * x[:, :head]
            l = l + f * ll
        merged[pl.ds(pl.multiple_of(g * pair_rows, 8), pair_rows), :] = o / l
        return carry

    lax.fori_loop(0, n_groups, merge_step, 0)
    attn = jnp.concatenate(
        [merged[pl.ds(n, own, stride=n_heads), :].astype(jnp.bfloat16) for n in range(n_heads)], axis=1)
    wo_copy.wait()
    for c in range(0, d_model, 512):
        proj[:, c:c + 512] = jnp.dot(attn, wo[:, c:c + 512], preferred_element_type=jnp.float32)

    swap = pltpu.make_async_remote_copy(proj, proj_in, proj_send, proj_recv,
                                        device_id={'tp': 1 - tp}, device_id_type=MESH)
    swap.start()
    swap.wait()
    sums[sp] = proj[...] + proj_in[...]

    def sum_copy(s):
        return pltpu.make_async_remote_copy(
            src_ref=sums.at[sp], dst_ref=sums.at[sp],
            send_sem=sum_send.at[s - 1], recv_sem=sum_recv.at[s - 1],
            device_id={'sp': lax.rem(sp + s, N_SP)}, device_id_type=MESH)

    for s in range(1, N_SP):
        sum_copy(s).start()
    for s in range(1, N_SP):
        sum_copy(s).wait()

    srow = lax.broadcasted_iota(jnp.int32, (GROUP, 1), 0)
    for g in range(n_groups):
        t = (2 * g) // GROUP * GROUP
        total = hidden[g * GROUP:(g + 1) * GROUP, :].astype(jnp.float32)
        gathered = jnp.zeros_like(total)
        for d in range(N_SP):
            x = sums[d, t:t + GROUP, :]
            shift = (2 * d - 2 * g) % GROUP
            if shift:
                x = pltpu.roll(x, shift, 0)
            gathered = jnp.where(srow // 2 == d, x, gathered)
        h_out[g * GROUP:(g + 1) * GROUP, :] = (total + gathered).astype(jnp.bfloat16)


def write_kernel(dims, pos, h_in, k_vm, v_vm, new_k, new_v, k_in, v_in, h_out, k_out, v_out,
                 slots, k_tile, v_tile, h_sem, rd_sem, wr_sem, k_sem, v_sem, k_row, v_row):
    n_seq, rows, kv, _, _, _ = dims
    sp = lax.axis_index('sp')
    seq_local = rows // kv
    n_held = HELD * GROUP
    per = 16 // kv
    sub = lax.broadcasted_iota(jnp.int32, (16, 1), 0) // kv
    held = ((k_vm, k_out, new_k, k_tile, k_sem, k_row), (v_vm, v_out, new_v, v_tile, v_sem, v_row))
    jobs = [(src, out, new, b) for src, out, new in ((k_in, k_out, new_k), (v_in, v_out, new_v))
            for b in range(n_held, n_seq, JOB)]

    def place(b):
        p = pos[b] - sp * seq_local
        blk = jnp.clip(p, 0, seq_local - 1) // per
        return pl.ds(pl.multiple_of(blk * 16, 16), 16), sub + blk * per == p

    def patched(ref, i, b, new):
        r, hit = place(b)
        fresh = new[pl.ds(pl.multiple_of(b * 16, 16), 16), :]
        return r, jnp.where(hit, fresh, ref[i, r, :].astype(jnp.float32)).astype(jnp.bfloat16)

    def read(j):
        src, _, _, b = jobs[j]
        return pltpu.make_async_copy(src.at[pl.ds(b, JOB)], slots.at[j % SLOTS], rd_sem.at[j])

    def write(j):
        _, out, _, b = jobs[j]
        return pltpu.make_async_copy(slots.at[j % SLOTS], out.at[pl.ds(b, JOB)], wr_sem.at[j])

    def block(vm, out, sem, g):
        s = pl.ds(g * GROUP, GROUP)
        return pltpu.make_async_copy(vm.at[s], out.at[s], sem.at[g])

    def run(j):
        _, _, new, b = jobs[j]
        slot = slots.at[j % SLOTS]
        read(j).wait()
        for i in range(JOB):
            r, x = patched(slot, i, b + i, new)
            slot[i, r, :] = x
        write(j).start()

    h_copy = pltpu.make_async_copy(h_in, h_out, h_sem)
    h_copy.start()
    for j in range(SLOTS):
        read(j).start()
    for vm, out, _, _, sem, _ in held:
        for g in range(HELD):
            block(vm, out, sem, g).start()
    for vm, _, new, tile, _, _ in held:
        def fill(b, carry):
            _, tile[b] = patched(vm, b, b, new)
            return carry

        lax.fori_loop(0, n_held, fill, 0)
    for j in range(len(jobs)):
        if j >= SLOTS:
            write(j - SLOTS).wait()
            read(j).start()
        if j < SLOTS:
            run(j)

    def row_copy(tile, out, row, b):
        r, _ = place(b)
        return pltpu.make_async_copy(tile.at[b], out.at[b, r], row.at[b])

    for n, (vm, out, _, tile, sem, row) in enumerate(held):
        def rows_out(g, carry):
            block(vm, out, sem, g).wait()
            for i in range(GROUP):
                row_copy(tile, out, row, g * GROUP + i).start()
            return carry

        lax.fori_loop(0, HELD, rows_out, 0)
        if n == 0:
            for j in range(SLOTS, len(jobs)):
                run(j)
    for _, out, _, tile, _, row in held:
        def drain(b, carry):
            row_copy(tile, out, row, b).wait()
            return carry

        lax.fori_loop(0, n_held, drain, 0)
    for j in range(SLOTS, len(jobs)):
        write(j).wait()
    h_copy.wait()


def solution(mesh):
    cache_spec = P('dp', 'sp', 'tp', None)

    def local_step(hidden, norm_scale, w_qkv, w_out, k_cache, v_cache, positions):
        n_seq, seq_local, kv, head = k_cache.shape
        d_model = hidden.shape[1]
        per_kv = w_qkv.shape[1] // (kv * head) - 2
        rows = seq_local * kv
        n_heads = kv * per_kv
        n_groups = n_seq // GROUP
        pair_rows = 2 * n_heads
        own = n_seq // N_SP
        n_jobs = 2 * (n_seq - HELD * GROUP) // JOB
        dims = (n_seq, rows, kv, head, per_kv, d_model)
        half = np.arange(head) % (head // 2)
        inv_freq = np.exp(half * (-2.0 * math.log(500000.0) / head)).astype(np.float32)
        sign = np.where(np.arange(head) < head // 2, -1.0, 1.0).astype(np.float32)
        angles = positions.astype(jnp.float32)[:, None] * inv_freq[None, :]
        cos2, sin2 = jnp.cos(angles), jnp.sin(angles) * sign
        f32, bf16 = jnp.float32, jnp.bfloat16
        vmem = pl.BlockSpec(memory_space=pltpu.VMEM)
        hbm = pl.BlockSpec(memory_space=pltpu.HBM)
        smem = pl.BlockSpec(memory_space=pltpu.SMEM)
        cache = (n_seq, rows, head)
        dma = pltpu.SemaphoreType.DMA
        keep = pltpu.with_memory_space_constraint
        w_qkv, w_out = keep(w_qkv, pltpu.HBM), keep(w_out, pltpu.HBM)
        k_flat = keep(k_cache.reshape(cache), pltpu.HBM)
        v_flat = keep(v_cache.reshape(cache), pltpu.HBM)
        h_vm, k_vm, v_vm, new_k, new_v = pl.pallas_call(
            lambda *refs: attend_kernel(dims, *refs),
            out_shape=(pltpu.VMEM(hidden.shape, bf16),
                       pltpu.VMEM((HELD * GROUP, rows, head), bf16),
                       pltpu.VMEM((HELD * GROUP, rows, head), bf16),
                       pltpu.VMEM((n_seq * 16, head), f32),
                       pltpu.VMEM((n_seq * 16, head), f32)),
            in_specs=[smem, vmem, vmem, vmem, vmem, hbm, hbm, hbm, hbm],
            out_specs=(vmem,) * 5,
            scratch_shapes=[
                pltpu.VMEM((W_CHUNKS, n_seq, d_model // W_CHUNKS), bf16),
                pltpu.VMEM((W_SLOTS, d_model // W_CHUNKS, w_qkv.shape[1]), bf16),
                pltpu.VMEM((n_seq, w_qkv.shape[1]), f32),
                pltpu.VMEM(w_out.shape, bf16),
                pltpu.VMEM((n_seq - HELD * GROUP, rows, head), bf16),
                pltpu.VMEM((n_seq - HELD * GROUP, rows, head), bf16),
                pltpu.VMEM((n_seq * n_heads, head), f32),
                pltpu.VMEM((n_seq * n_heads, head), f32),
                pltpu.VMEM((n_seq * n_heads, head), f32),
                pltpu.VMEM((pair_rows, rows), jnp.int32),
                pltpu.VMEM((n_groups, N_SP, pair_rows, 2 * head), f32),
                pltpu.VMEM((n_groups, N_SP - 1, pair_rows, 2 * head), f32),
                pltpu.VMEM((own * n_heads, head), f32),
                pltpu.VMEM((own, d_model), f32),
                pltpu.VMEM((own, d_model), f32),
                pltpu.VMEM((N_SP, own, d_model), f32),
                dma((W_CHUNKS,)), dma, dma((n_groups,)), dma((n_groups,)),
                dma((n_groups, N_SP - 1)), dma((n_groups, N_SP - 1)),
                dma, dma, dma((N_SP - 1,)), dma((N_SP - 1,)),
            ],
            compiler_params=pltpu.CompilerParams(
                collective_id=0, has_side_effects=True, vmem_limit_bytes=33 * MIB),
            name='attend',
        )(positions, hidden, norm_scale.reshape(1, d_model), cos2, sin2, w_qkv, w_out, k_flat, v_flat)
        h_out, k_out, v_out = pl.pallas_call(
            lambda *refs: write_kernel(dims, *refs),
            out_shape=(jax.ShapeDtypeStruct(hidden.shape, bf16),
                       jax.ShapeDtypeStruct(cache, bf16), jax.ShapeDtypeStruct(cache, bf16)),
            in_specs=[smem] + [vmem] * 5 + [hbm] * 2,
            out_specs=(hbm,) * 3,
            scratch_shapes=[
                pltpu.VMEM((SLOTS, JOB, rows, head), bf16),
                pltpu.VMEM((HELD * GROUP, 16, head), bf16),
                pltpu.VMEM((HELD * GROUP, 16, head), bf16),
                dma, dma((n_jobs,)), dma((n_jobs,)), dma((HELD,)), dma((HELD,)),
                dma((HELD * GROUP,)), dma((HELD * GROUP,)),
            ],
            compiler_params=pltpu.CompilerParams(vmem_limit_bytes=W_VMEM * MIB),
            name='write',
        )(positions, *[keep(x, pltpu.VMEM) for x in (h_vm, k_vm, v_vm, new_k, new_v)], k_flat, v_flat)
        return h_out, k_out.reshape(k_cache.shape), v_out.reshape(v_cache.shape)

    return jax.shard_map(
        local_step,
        mesh=mesh,
        in_specs=(P('dp', None), P(None), P(None, 'tp'), P('tp', None), cache_spec, cache_spec, P('dp')),
        out_specs=(P('dp', None), cache_spec, cache_spec),
        check_vma=False,
    )
```

time: 164 us -> 70.2 us (0.43)
  Pallas kernels: 0 us -> 65.8 us
  waiting for transfers between devices: 60 us -> 0 us
  other arithmetic: 35.9 us -> 2.16 us
  matrix products: 33.3 us -> 0 us
  blocking collectives: 15 us -> 0 us
  between operations: 14.2 us -> 0.65 us
  local copies, waits for them, and re-layouts: 5.28 us -> 1.3 us
    pallas_call x0 -> x2, Pallas kernels: none -> 65.8 us  [the longest x1 50.6 us: local_step(): pl.pallas_call(lambda *refs: attend_kernel(dims, *refs), out_shape=(pltpu...]
    psum x2 -> x0, waiting for transfers between devices: 60 us -> none  [the longest x1 31 us: local_step(): merged = lax.psum(packed, 'sp')]
    dot_general x4 -> x0, matrix products: 33.3 us -> none  [the longest x1 10.4 us: local_step(): jnp.einsum('bgqd,bsgd->bgqs', queries, k_upd, preferred_element_type=jnp....]
    select_n x1 -> x0, other arithmetic: 25.9 us -> none  [local_step(): v_upd = jnp.where(new_row, grouped[:, :, q_per_kv + 1][:, None], v_cache)]
    pmax x1 -> x0, blocking collectives: 15 us -> none  [local_step(): global_max = lax.pmax(local_max, 'sp')]
    convert_element_type x5 -> x1, other arithmetic: 4.14 us -> 0.66 us  [local_step(): angles = positions.astype(jnp.float32)[:, None] * inv_freq[None, :]]
    reduce_sum x3 -> x0, other arithmetic: 3.24 us -> none  [the longest x1 1.27 us: layer_norm_bf16(): row_var = jnp.mean(centered * centered, axis=-1, keepdims=True)]
    concatenate x2 -> x0, other arithmetic: 1.82 us -> none  [the longest x1 1.32 us: local_step(): jnp.concatenate([local_out * factor[..., None], (local_sum * factor)[...,...]
  transfers between devices with their start and end apart: 2 -> 0, of which waited for: 2 -> 0; matrix products, arithmetic and copies ran while one was open for 0% -> 0% of each run, Pallas kernels for 0% -> 0%
where the time goes in v1:
time: 70.2 us; the launch traced here: 69.9 us
  Pallas kernels  65.8 us (94%)
  other arithmetic  2.16 us (3%)
  local copies, waits for them, and re-layouts  1.3 us (2%)
    pallas_call x1, Pallas kernels, local_step(): pl.pallas_call(lambda *refs: attend_kernel(dims, *refs), out_shape=(pltpu...  50.6 us
    pallas_call x1, Pallas kernels, local_step(): pl.pallas_call(lambda *refs: write_kernel(dims, *refs), out_shape=(jax.Sh...  15.2 us
    mul x1, other arithmetic, local_step(): cos2, sin2 = (jnp.cos(angles), jnp.sin(angles) * sign)  1.5 us

profile of v1, /device:TPU:0, one launch (start us, length us, event | category | flops | bytes accessed | tf_op | source)
XLA Modules:
  0.0 69.9 jit_solution(4209529268856349301)
XLA Ops:
  0.6 0.7 convert_element_type.3
  1.3 1.3 %reshape.23.refs_2_ = bf16[1,3072]{1,0:T(2,128)(2,1)} reshape(bf16[3072]{0:T(1024)(128)(2,1)} %param.10) | data formatting | bytes 12288 | tf_op jit(solution)/shard_map/reshape | solution.py:368
  2.6 1.5 %fusion = (f32[64,128]{1,0:T(8,128)}, f32[64,128]{1,0:T(8,128)}) fusion(f32[128]{0:T(128)} %constant.5.clone, f32[128]{0:T(128)} %constant.6, f32[64]{0:T(128)S(1)} %convert_element_type.3), kind=kLoop, calls=%fused_computation.2 | loop fusion | flops 16384 | bytes 66816 | tf_op jit(solution)/shard_map/mul | solution.py:324
  4.1 0.0 copy-start
  4.1 50.6 %attend.1 = (bf16[64,3072]{1,0:T(8,128)(2,1)S(1)}, bf16[56,1024,128]{2,1,0:T(8,128)(2,1)S(1)}, bf16[56,1024,128]{2,1,0:T(8,128)(2,1)S(1)}, f32[1024,128]{1,0:T(8,128)S(1)}, f32[1024,128]{1,0:T(8,128)S(1)}) custom-call(s32[64]{0:T(128)} %refs_0_.3, bf16[64,3072]{1,0:T(8,128)(2,1)} %refs_1_.1, bf16[1,3072]{1,0:T(2,128)(2,1)} %reshape.23.refs_2_, ...), custom_call_target="tpu_custom_call" | custom-call | tf_op jit(solution)/shard_map/attend/pallas_call | solution.py:335
  54.7 0.0 copy-done
  54.7 15.2 %write.1 = (bf16[64,3072]{1,0:T(8,128)(2,1)}, bf16[64,1024,128]{2,1,0:T(8,128)(2,1)}, bf16[64,1024,128]{2,1,0:T(8,128)(2,1)}) custom-call(s32[64]{0:T(128)S(1)} %copy-done, bf16[64,3072]{1,0:T(8,128)(2,1)S(1)} %get-tuple-element.11.refs_1_, bf16[56,1024,128]{2,1,0:T(8,128)(2,1)S(1)} %get-tuple-element.12.refs_2_, ...), custom_call_target="tpu_custom_call" | custom-call | tf_op jit(solution)/shard_map/write/pallas_call | solution.py:369
Async XLA Ops:
  4.1 50.6 %copy-start = (s32[64]{0:T(128)S(1)}, s32[64]{0:T(128)}, u32[]{:S(2)}) copy-start(s32[64]{0:T(128)} %refs_0_.3) | copy-start | bytes 772

commit v2 on v1

--- a/solution.py
+++ b/solution.py
@@ -14,15 +14,17 @@
 GROUP = 8
 W_CHUNKS = 6
 W_SLOTS = 3
+AHEAD = 3
 HELD = 7
 JOB = 2
 SLOTS = 4
+WINDOW = 4
 W_VMEM = 3
 
 
-def attend_kernel(dims, pos, hidden, norm_scale, cos2, sin2, w_qkv, w_out, k_in, v_in,
+def attend_kernel(dims, pos, hidden, norm_scale, inv_freq, w_qkv, w_out, k_in, v_in,
                   h_out, k_vm, v_vm, new_k, new_v,
-                  u, wq, acc, wo, k_rest, v_rest, q_rows, kn_rows, vn_rows, tok, part, recv, merged, proj, proj_in, sums,
+                  u, wq, acc, rope_c, rope_s, wo, k_rest, v_rest, q_rows, kn_rows, vn_rows, tok, part, recv, merged, proj, proj_in, sums,
                   w_sem, wo_sem, k_sem, v_sem, part_send, part_recv, proj_send, proj_recv, sum_send, sum_recv):
     n_seq, rows, kv, head, per_kv, d_model = dims
     n_heads = kv * per_kv
@@ -51,12 +53,13 @@
     def v_copy(g):
         return cache_copy(v_in, v_vm, v_rest, HELD, v_sem, g)
 
+    def fetch(g):
+        k_copy(g).start()
+        v_copy(g).start()
+
     wo_copy = pltpu.make_async_copy(w_out, wo, wo_sem)
     for c in range(W_SLOTS):
         w_copy(c).start()
-    for g in range(n_groups - W_CHUNKS):
-        k_copy(g).start()
-        v_copy(g).start()
 
     barrier = pltpu.get_barrier_semaphore()
     for s in range(1, N_SP):
@@ -67,7 +70,9 @@
     mean = jnp.mean(hid, axis=-1, keepdims=True)
     cen = hid - mean
     var = jnp.mean(cen * cen, axis=-1, keepdims=True)
-    normed = (cen * lax.rsqrt(var + 1e-5) * norm_scale[...].astype(jnp.float32)).astype(jnp.bfloat16)
+    scale_rows = norm_scale[...].astype(jnp.float32)
+    scale_row = jnp.concatenate([scale_rows[i:i + 1] for i in range(scale_rows.shape[0])], axis=1)
+    normed = (cen * lax.rsqrt(var + 1e-5) * scale_row).astype(jnp.bfloat16)
     for c in range(W_CHUNKS):
         u[c] = normed[:, c * w_rows:(c + 1) * w_rows]
 
@@ -78,19 +83,27 @@
 
     acc[...] = jnp.zeros_like(acc)
 
+    brow = lax.broadcasted_iota(jnp.int32, (n_seq, 1), 0)
+    pos_col = jnp.zeros((n_seq, 1), jnp.int32)
+    for b in range(n_seq):
+        pos_col = jnp.where(brow == b, pos[b], pos_col)
+    angles = pos_col.astype(jnp.float32) * inv_freq[...]
+    c2 = jnp.cos(angles)
+    s2 = jnp.sin(angles)
+    s2 = jnp.where(lax.broadcasted_iota(jnp.int32, s2.shape, 1) < head // 2, -s2, s2)
+    rope_c[...] = c2
+    rope_s[...] = s2
+
     for c in range(W_CHUNKS):
         w_copy(c).wait()
-        g = c + (n_groups - W_CHUNKS)
-        k_copy(g).start()
-        v_copy(g).start()
         acc[...] += jnp.dot(u[c], wq[c % W_SLOTS], preferred_element_type=jnp.float32)
         if c + W_SLOTS < W_CHUNKS:
             w_copy(c + W_SLOTS).start()
-
-    wo_copy.start()
-
-    c2 = cos2[...]
-    s2 = sin2[...]
+        else:
+            fetch(c + W_SLOTS - W_CHUNKS)
+
+    c2 = rope_c[...]
+    s2 = rope_s[...]
     for g in range(kv):
         for j in range(per_kv + 2):
             lo = (g * (per_kv + 2) + j) * head
@@ -141,16 +154,21 @@
             part_copy(g, s).start()
 
     def held_step(g, carry):
-        s = pl.ds(g * GROUP, GROUP)
-        pltpu.make_async_copy(k_in.at[s], k_vm.at[s], k_sem.at[g]).wait()
-        pltpu.make_async_copy(v_in.at[s], v_vm.at[s], v_sem.at[g]).wait()
+        for src, dst, sem in ((k_in, k_vm, k_sem), (v_in, v_vm, v_sem)):
+            now, later = pl.ds(g * GROUP, GROUP), pl.ds((g + AHEAD) * GROUP, GROUP)
+            pltpu.make_async_copy(src.at[now], dst.at[now], sem.at[g]).wait()
+            pltpu.make_async_copy(src.at[later], dst.at[later], sem.at[g + AHEAD]).start()
         group_step(g, k_vm, v_vm, 0, 0)
         return carry
 
-    lax.fori_loop(0, HELD, held_step, 0)
-    for g in range(HELD, n_groups):
+    lax.fori_loop(0, HELD - AHEAD, held_step, 0)
+    for g in range(HELD - AHEAD, n_groups):
         k_copy(g).wait()
         v_copy(g).wait()
+        if g + AHEAD < n_groups:
+            fetch(g + AHEAD)
+        elif g + AHEAD == n_groups:
+            wo_copy.start()
         k_ref, ki = held(k_vm, k_rest, HELD, g)
         v_ref, vi = held(v_vm, v_rest, HELD, g)
         group_step(g, k_ref, v_ref, (g - ki) * GROUP, (g - vi) * GROUP)
@@ -214,27 +232,23 @@
         h_out[g * GROUP:(g + 1) * GROUP, :] = (total + gathered).astype(jnp.bfloat16)
 
 
-def write_kernel(dims, pos, h_in, k_vm, v_vm, new_k, new_v, k_in, v_in, h_out, k_out, v_out,
-                 slots, k_tile, v_tile, h_sem, rd_sem, wr_sem, k_sem, v_sem, k_row, v_row):
+def write_kernel(dims, pos, h_in, k_vm, v_vm, new_k, new_v, k_in, v_in, h_out, k_out, v_out, k_same, v_same,
+                 slots, h_sem, rd_sem, wr_sem, blk_sem):
     n_seq, rows, kv, _, _, _ = dims
     sp = lax.axis_index('sp')
     seq_local = rows // kv
     n_held = HELD * GROUP
     per = 16 // kv
     sub = lax.broadcasted_iota(jnp.int32, (16, 1), 0) // kv
-    held = ((k_vm, k_out, new_k, k_tile, k_sem, k_row), (v_vm, v_out, new_v, v_tile, v_sem, v_row))
     jobs = [(src, out, new, b) for src, out, new in ((k_in, k_out, new_k), (v_in, v_out, new_v))
             for b in range(n_held, n_seq, JOB)]
 
-    def place(b):
+    def patch(ref, i, b, new):
         p = pos[b] - sp * seq_local
         blk = jnp.clip(p, 0, seq_local - 1) // per
-        return pl.ds(pl.multiple_of(blk * 16, 16), 16), sub + blk * per == p
-
-    def patched(ref, i, b, new):
-        r, hit = place(b)
+        r = pl.ds(pl.multiple_of(blk * 16, 16), 16)
         fresh = new[pl.ds(pl.multiple_of(b * 16, 16), 16), :]
-        return r, jnp.where(hit, fresh, ref[i, r, :].astype(jnp.float32)).astype(jnp.bfloat16)
+        ref[i, r, :] = jnp.where(sub + blk * per == p, fresh, ref[i, r, :].astype(jnp.float32)).astype(jnp.bfloat16)
 
     def read(j):
         src, _, _, b = jobs[j]
@@ -244,61 +258,48 @@
         _, out, _, b = jobs[j]
         return pltpu.make_async_copy(slots.at[j % SLOTS], out.at[pl.ds(b, JOB)], wr_sem.at[j])
 
-    def block(vm, out, sem, g):
-        s = pl.ds(g * GROUP, GROUP)
-        return pltpu.make_async_copy(vm.at[s], out.at[s], sem.at[g])
-
     def run(j):
         _, _, new, b = jobs[j]
-        slot = slots.at[j % SLOTS]
         read(j).wait()
         for i in range(JOB):
-            r, x = patched(slot, i, b + i, new)
-            slot[i, r, :] = x
+            patch(slots.at[j % SLOTS], i, b + i, new)
         write(j).start()
 
+    def again(j):
+        write(j - SLOTS).wait()
+        read(j).start()
+
+    def block(n):
+        vm, out = ((k_vm, k_out), (v_vm, v_out))[n % 2]
+        s = pl.ds(n // 2 * GROUP, GROUP)
+        return pltpu.make_async_copy(vm.at[s], out.at[s], blk_sem.at[n])
+
+    def send(n):
+        vm, new = ((k_vm, new_k), (v_vm, new_v))[n % 2]
+        for i in range(GROUP):
+            b = n // 2 * GROUP + i
+            patch(vm, b, b, new)
+        block(n).start()
+
+    n_blocks = 2 * HELD
     h_copy = pltpu.make_async_copy(h_in, h_out, h_sem)
     h_copy.start()
     for j in range(SLOTS):
         read(j).start()
-    for vm, out, _, _, sem, _ in held:
-        for g in range(HELD):
-            block(vm, out, sem, g).start()
-    for vm, _, new, tile, _, _ in held:
-        def fill(b, carry):
-            _, tile[b] = patched(vm, b, b, new)
-            return carry
-
-        lax.fori_loop(0, n_held, fill, 0)
-    for j in range(len(jobs)):
-        if j >= SLOTS:
-            write(j - SLOTS).wait()
-            read(j).start()
-        if j < SLOTS:
-            run(j)
-
-    def row_copy(tile, out, row, b):
-        r, _ = place(b)
-        return pltpu.make_async_copy(tile.at[b], out.at[b, r], row.at[b])
-
-    for n, (vm, out, _, tile, sem, row) in enumerate(held):
-        def rows_out(g, carry):
-            block(vm, out, sem, g).wait()
-            for i in range(GROUP):
-                row_copy(tile, out, row, g * GROUP + i).start()
-            return carry
-
-        lax.fori_loop(0, HELD, rows_out, 0)
-        if n == 0:
-            for j in range(SLOTS, len(jobs)):
+    for n in range(n_blocks):
+        if n >= WINDOW:
+            block(n - WINDOW).wait()
+        send(n)
+        for j in range(len(jobs)):
+            if j < SLOTS and n == WINDOW + j // 2 - 1:
                 run(j)
-    for _, out, _, tile, _, row in held:
-        def drain(b, carry):
-            row_copy(tile, out, row, b).wait()
-            return carry
-
-        lax.fori_loop(0, n_held, drain, 0)
-    for j in range(SLOTS, len(jobs)):
+            if j >= SLOTS and n == WINDOW + 2 + j // 2:
+                again(j)
+            if j >= SLOTS and n == WINDOW + 4 + j // 2:
+                run(j)
+    for n in range(n_blocks - WINDOW, n_blocks):
+        block(n).wait()
+    for j in range(len(jobs) - SLOTS, len(jobs)):
         write(j).wait()
     h_copy.wait()
 
@@ -318,10 +319,7 @@
         n_jobs = 2 * (n_seq - HELD * GROUP) // JOB
         dims = (n_seq, rows, kv, head, per_kv, d_model)
         half = np.arange(head) % (head // 2)
-        inv_freq = np.exp(half * (-2.0 * math.log(500000.0) / head)).astype(np.float32)
-        sign = np.where(np.arange(head) < head // 2, -1.0, 1.0).astype(np.float32)
-        angles = positions.astype(jnp.float32)[:, None] * inv_freq[None, :]
-        cos2, sin2 = jnp.cos(angles), jnp.sin(angles) * sign
+        inv_freq = np.exp(half * (-2.0 * math.log(500000.0) / head)).astype(np.float32)[None]
         f32, bf16 = jnp.float32, jnp.bfloat16
         vmem = pl.BlockSpec(memory_space=pltpu.VMEM)
         hbm = pl.BlockSpec(memory_space=pltpu.HBM)
@@ -339,12 +337,14 @@
                        pltpu.VMEM((HELD * GROUP, rows, head), bf16),
                        pltpu.VMEM((n_seq * 16, head), f32),
                        pltpu.VMEM((n_seq * 16, head), f32)),
-            in_specs=[smem, vmem, vmem, vmem, vmem, hbm, hbm, hbm, hbm],
+            in_specs=[smem, vmem, vmem, vmem, hbm, hbm, hbm, hbm],
             out_specs=(vmem,) * 5,
             scratch_shapes=[
                 pltpu.VMEM((W_CHUNKS, n_seq, d_model // W_CHUNKS), bf16),
                 pltpu.VMEM((W_SLOTS, d_model // W_CHUNKS, w_qkv.shape[1]), bf16),
                 pltpu.VMEM((n_seq, w_qkv.shape[1]), f32),
+                pltpu.VMEM((n_seq, head), f32),
+                pltpu.VMEM((n_seq, head), f32),
                 pltpu.VMEM(w_out.shape, bf16),
                 pltpu.VMEM((n_seq - HELD * GROUP, rows, head), bf16),
                 pltpu.VMEM((n_seq - HELD * GROUP, rows, head), bf16),
@@ -365,19 +365,18 @@
             compiler_params=pltpu.CompilerParams(
                 collective_id=0, has_side_effects=True, vmem_limit_bytes=33 * MIB),
             name='attend',
-        )(positions, hidden, norm_scale.reshape(1, d_model), cos2, sin2, w_qkv, w_out, k_flat, v_flat)
-        h_out, k_out, v_out = pl.pallas_call(
+        )(positions, hidden, norm_scale.reshape(d_model // 128, 128), inv_freq, w_qkv, w_out, k_flat, v_flat)
+        h_out, k_out, v_out, _, _ = pl.pallas_call(
             lambda *refs: write_kernel(dims, *refs),
             out_shape=(jax.ShapeDtypeStruct(hidden.shape, bf16),
-                       jax.ShapeDtypeStruct(cache, bf16), jax.ShapeDtypeStruct(cache, bf16)),
+                       jax.ShapeDtypeStruct(cache, bf16), jax.ShapeDtypeStruct(cache, bf16),
+                       pltpu.VMEM(k_vm.shape, bf16), pltpu.VMEM(v_vm.shape, bf16)),
             in_specs=[smem] + [vmem] * 5 + [hbm] * 2,
-            out_specs=(hbm,) * 3,
+            out_specs=(hbm,) * 3 + (vmem,) * 2,
+            input_output_aliases={2: 3, 3: 4},
             scratch_shapes=[
                 pltpu.VMEM((SLOTS, JOB, rows, head), bf16),
-                pltpu.VMEM((HELD * GROUP, 16, head), bf16),
-                pltpu.VMEM((HELD * GROUP, 16, head), bf16),
-                dma, dma((n_jobs,)), dma((n_jobs,)), dma((HELD,)), dma((HELD,)),
-                dma((HELD * GROUP,)), dma((HELD * GROUP,)),
+                dma, dma((n_jobs,)), dma((n_jobs,)), dma((2 * HELD,)),
             ],
             compiler_params=pltpu.CompilerParams(vmem_limit_bytes=W_VMEM * MIB),
             name='write',

time: 70.2 us -> 58.6 us (0.83)
  Pallas kernels: 65.8 us -> 57.7 us
  other arithmetic: 2.16 us -> 0 us
  local copies, waits for them, and re-layouts: 1.3 us -> 0.01 us
    pallas_call x1, Pallas kernels: 50.6 us -> 45 us  [local_step(): pl.pallas_call(lambda *refs: attend_kernel(dims, *refs), out_shape=(pltpu...]
    pallas_call x1, Pallas kernels: 15.2 us -> 12.8 us  [local_step(): pl.pallas_call(lambda *refs: write_kernel(dims, *refs), out_shape=(jax.Sh...]
    mul x1 -> x0, other arithmetic: 1.5 us -> none  [local_step(): cos2, sin2 = (jnp.cos(angles), jnp.sin(angles) * sign)]
    reshape x1 -> x0, local copies, waits for them, and re-layouts: 1.3 us -> none  [local_step(): norm_scale.reshape(1, d_model)]
where the time goes in v2:
time: 58.6 us; the launch traced here: 58.4 us
  Pallas kernels  57.7 us (98%)
  between operations  0.66 us (1%)
    pallas_call x1, Pallas kernels, local_step(): pl.pallas_call(lambda *refs: attend_kernel(dims, *refs), out_shape=(pltpu...  45 us
    pallas_call x1, Pallas kernels, local_step(): pl.pallas_call(lambda *refs: write_kernel(dims, *refs), out_shape=(jax.Sh...  12.8 us

profile of v2, /device:TPU:0, one launch (start us, length us, event | category | flops | bytes accessed | tf_op | source)
XLA Modules:
  0.0 58.4 jit_solution(17688444171297089975)
XLA Ops:
  0.6 0.0 copy-start
  0.6 45.0 %attend.1 = (bf16[64,3072]{1,0:T(8,128)(2,1)S(1)}, bf16[56,1024,128]{2,1,0:T(8,128)(2,1)S(1)}, bf16[56,1024,128]{2,1,0:T(8,128)(2,1)S(1)}, f32[1024,128]{1,0:T(8,128)S(1)}, f32[1024,128]{1,0:T(8,128)S(1)}) custom-call(s32[64]{0:T(128)} %refs_0_.3, bf16[64,3072]{1,0:T(8,128)(2,1)} %refs_1_.1, bf16[24,128]{1,0:T(8,128)(2,1)} %bitcast.9, ...), custom_call_target="tpu_custom_call" | custom-call | tf_op jit(solution)/shard_map/attend/pallas_call | solution.py:333
  45.6 0.0 copy-done
  45.6 12.8 %write.1 = (bf16[64,3072]{1,0:T(8,128)(2,1)}, bf16[64,1024,128]{2,1,0:T(8,128)(2,1)}, bf16[64,1024,128]{2,1,0:T(8,128)(2,1)}, bf16[56,1024,128]{2,1,0:T(8,128)(2,1)S(1)}, bf16[56,1024,128]{2,1,0:T(8,128)(2,1)S(1)}) custom-call(s32[64]{0:T(128)S(1)} %copy-done, ...), custom_call_target="tpu_custom_call", output_to_operand_aliasing={{3}: (2, {}), {4}: (3, {})} | custom-call | tf_op jit(solution)/shard_map/write/pallas_call | solution.py:369
Async XLA Ops:
  0.6 45.0 %copy-start = (s32[64]{0:T(128)S(1)}, s32[64]{0:T(128)}, u32[]{:S(2)}) copy-start(s32[64]{0:T(128)} %refs_0_.3) | copy-start | bytes 772

commit v3 on v2

--- a/solution.py
+++ b/solution.py
@@ -11,6 +11,8 @@
 NEG = -1e30
 MIB = 1024 * 1024
 N_SP = 4
+COLS = 4
+WO_AT = 7
 GROUP = 8
 W_CHUNKS = 6
 W_SLOTS = 3
@@ -24,8 +26,9 @@
 
 def attend_kernel(dims, pos, hidden, norm_scale, inv_freq, w_qkv, w_out, k_in, v_in,
                   h_out, k_vm, v_vm, new_k, new_v,
-                  u, wq, acc, rope_c, rope_s, wo, k_rest, v_rest, q_rows, kn_rows, vn_rows, tok, part, recv, merged, proj, proj_in, sums,
-                  w_sem, wo_sem, k_sem, v_sem, part_send, part_recv, proj_send, proj_recv, sum_send, sum_recv):
+                  u, wq, acc, rope_c, rope_s, wo, k_rest, v_rest, q_rows, kn_rows, vn_rows, tok, score, part, recv, merged, proj, proj_in, sums,
+                  w_sem, wo_sem, k_sem, v_sem, part_send, part_recv, tp_send, tp_recv, x_send, x_recv,
+                  core_send, core_recv, fwd_send, fwd_recv):
     n_seq, rows, kv, head, per_kv, d_model = dims
     n_heads = kv * per_kv
     n_groups = n_seq // GROUP
@@ -131,47 +134,62 @@
             send_sem=part_send.at[g, s - 1], recv_sem=part_recv.at[g, s - 1],
             device_id={'sp': dst}, device_id_type=MESH)
 
-    def group_step(g, k_ref, v_ref, k_off, v_off):
+    lane = lax.broadcasted_iota(jnp.int32, (8, head), 1)
+    n_stat = pair_rows // 8
+
+    def scores(g, k_ref, k_off):
         for d in range(N_SP):
-            b = g * GROUP + 2 * d
-            kb, vb = b - k_off, b - v_off
+            kb = g * GROUP + 2 * d - k_off
             q = q_rows[pl.ds(pl.multiple_of((g * N_SP + d) * pair_rows, 8), pair_rows), :]
             zero = jnp.zeros_like(q)
             q_blk = jnp.concatenate([jnp.where(first, q, zero), jnp.where(first, zero, q)], axis=1).astype(jnp.bfloat16)
             k_cat = jnp.concatenate([k_ref[kb], k_ref[kb + 1]], axis=1)
-            s = lax.dot_general(q_blk, k_cat, (((1,), (1,)), ((), ())), preferred_element_type=jnp.float32)
+            score[d] = lax.dot_general(q_blk, k_cat, (((1,), (1,)), ((), ())), preferred_element_type=jnp.float32)
+
+    def values(g, v_ref, v_off):
+        for d in range(N_SP):
+            b = g * GROUP + 2 * d
+            vb = b - v_off
             limit = jnp.where(first, pos[b], pos[b + 1])
-            s = jnp.where(tok[...] < limit, s, NEG)
+            s = jnp.where(tok[...] < limit, score[d], NEG)
             m = jnp.max(s, axis=-1, keepdims=True)
             w = jnp.exp2((s - m) * scale2)
             l = jnp.sum(w, axis=-1, keepdims=True)
             v_cat = jnp.concatenate([v_ref[vb], v_ref[vb + 1]], axis=1)
             o = jnp.dot(w.astype(jnp.bfloat16), v_cat, preferred_element_type=jnp.float32)
-            part[g, d, :, :head] = jnp.where(first, o[:, :head], o[:, head:])
-            lane = lax.broadcasted_iota(jnp.int32, (pair_rows, head), 1)
-            part[g, d, :, head:] = jnp.where(lane < head // 2, m, l)
+            part[g, d, :pair_rows] = jnp.where(first, o[:, :head], o[:, head:])
+            stat = jnp.zeros((8, head), jnp.float32)
+            for i in range(n_stat):
+                stat = jnp.where(lane == i, m[8 * i:8 * i + 8], stat)
+                stat = jnp.where(lane == n_stat + i, l[8 * i:8 * i + 8], stat)
+            part[g, d, pair_rows:] = stat
         for s in range(1, N_SP):
             part_copy(g, s).start()
 
     def held_step(g, carry):
-        for src, dst, sem in ((k_in, k_vm, k_sem), (v_in, v_vm, v_sem)):
-            now, later = pl.ds(g * GROUP, GROUP), pl.ds((g + AHEAD) * GROUP, GROUP)
-            pltpu.make_async_copy(src.at[now], dst.at[now], sem.at[g]).wait()
-            pltpu.make_async_copy(src.at[later], dst.at[later], sem.at[g + AHEAD]).start()
-        group_step(g, k_vm, v_vm, 0, 0)
+        now, later = pl.ds(g * GROUP, GROUP), pl.ds((g + AHEAD) * GROUP, GROUP)
+        pltpu.make_async_copy(k_in.at[now], k_vm.at[now], k_sem.at[g]).wait()
+        pltpu.make_async_copy(k_in.at[later], k_vm.at[later], k_sem.at[g + AHEAD]).start()
+        scores(g, k_vm, 0)
+        pltpu.make_async_copy(v_in.at[now], v_vm.at[now], v_sem.at[g]).wait()
+        pltpu.make_async_copy(v_in.at[later], v_vm.at[later], v_sem.at[g + AHEAD]).start()
+        values(g, v_vm, 0)
         return carry
 
     lax.fori_loop(0, HELD - AHEAD, held_step, 0)
     for g in range(HELD - AHEAD, n_groups):
+        k_ref, ki = held(k_vm, k_rest, HELD, g)
+        v_ref, vi = held(v_vm, v_rest, HELD, g)
         k_copy(g).wait()
+        if g + AHEAD < n_groups:
+            k_copy(g + AHEAD).start()
+        scores(g, k_ref, (g - ki) * GROUP)
         v_copy(g).wait()
         if g + AHEAD < n_groups:
-            fetch(g + AHEAD)
-        elif g + AHEAD == n_groups:
+            v_copy(g + AHEAD).start()
+        if g == WO_AT:
             wo_copy.start()
-        k_ref, ki = held(k_vm, k_rest, HELD, g)
-        v_ref, vi = held(v_vm, v_rest, HELD, g)
-        group_step(g, k_ref, v_ref, (g - ki) * GROUP, (g - vi) * GROUP)
+        values(g, v_ref, (g - vi) * GROUP)
 
     def merge_step(g, carry):
         for s in range(1, N_SP):
@@ -179,8 +197,13 @@
         r = pl.ds(pl.multiple_of((g * N_SP + sp) * pair_rows, 8), pair_rows)
         s_new = jnp.sum(q_rows[r, :] * kn_rows[r, :], axis=-1, keepdims=True)
         outs = [part[g, sp]] + [recv[g, s] for s in range(N_SP - 1)]
-        ms = [x[:, head:head + 1] for x in outs]
-        ls = [x[:, head + head // 2:head + head // 2 + 1] for x in outs]
+
+        def column(x, first_lane):
+            return jnp.concatenate(
+                [x[pair_rows:, first_lane + i:first_lane + i + 1] for i in range(n_stat)], axis=0)
+
+        ms = [column(x, 0) for x in outs]
+        ls = [column(x, n_stat) for x in outs]
         top = s_new
         for m in ms:
             top = jnp.maximum(top, m)
@@ -189,7 +212,7 @@
         l = f
         for x, m, ll in zip(outs, ms, ls):
             f = jnp.exp2((m - top) * scale2)
-            o = o + f * x[:, :head]
+            o = o + f * x[:pair_rows]
             l = l + f * ll
         merged[pl.ds(pl.multiple_of(g * pair_rows, 8), pair_rows), :] = o / l
         return carry
@@ -198,38 +221,54 @@
     attn = jnp.concatenate(
         [merged[pl.ds(n, own, stride=n_heads), :].astype(jnp.bfloat16) for n in range(n_heads)], axis=1)
     wo_copy.wait()
-    for c in range(0, d_model, 512):
-        proj[:, c:c + 512] = jnp.dot(attn, wo[:, c:c + 512], preferred_element_type=jnp.float32)
-
-    swap = pltpu.make_async_remote_copy(proj, proj_in, proj_send, proj_recv,
-                                        device_id={'tp': 1 - tp}, device_id_type=MESH)
-    swap.start()
-    swap.wait()
-    sums[sp] = proj[...] + proj_in[...]
-
-    def sum_copy(s):
-        return pltpu.make_async_remote_copy(
-            src_ref=sums.at[sp], dst_ref=sums.at[sp],
-            send_sem=sum_send.at[s - 1], recv_sem=sum_recv.at[s - 1],
-            device_id={'sp': lax.rem(sp + s, N_SP)}, device_id_type=MESH)
-
-    for s in range(1, N_SP):
-        sum_copy(s).start()
-    for s in range(1, N_SP):
-        sum_copy(s).wait()
+    width = d_model // COLS
+    partner = sp + 1 - 2 * lax.rem(sp, 2)
+    across = lax.rem(sp + 2, N_SP)
+
+    def tp_copy(c):
+        return pltpu.make_async_remote_copy(proj.at[c], proj_in.at[c], tp_send.at[c], tp_recv.at[c],
+                                            device_id={'tp': 1 - tp}, device_id_type=MESH)
+
+    def x_copy(c):
+        return pltpu.make_async_remote_copy(sums.at[c, sp], sums.at[c, sp], x_send.at[c], x_recv.at[c],
+                                            device_id={'sp': across}, device_id_type=MESH)
+
+    def core_copy(c):
+        return pltpu.make_async_remote_copy(sums.at[c, sp], sums.at[c, sp], core_send.at[c], core_recv.at[c],
+                                            device_id={'sp': partner}, device_id_type=MESH)
+
+    def fwd_copy(c):
+        return pltpu.make_async_remote_copy(sums.at[c, across], sums.at[c, across], fwd_send.at[c], fwd_recv.at[c],
+                                            device_id={'sp': partner}, device_id_type=MESH)
+
+    for c in range(COLS):
+        proj[c] = jnp.dot(attn, wo[:, c * width:(c + 1) * width], preferred_element_type=jnp.float32)
+        tp_copy(c).start()
+    for c in range(COLS):
+        tp_copy(c).wait()
+        sums[c, sp] = proj[c] + proj_in[c]
+        x_copy(c).start()
+        core_copy(c).start()
+    for c in range(COLS):
+        x_copy(c).wait()
+        fwd_copy(c).start()
 
     srow = lax.broadcasted_iota(jnp.int32, (GROUP, 1), 0)
-    for g in range(n_groups):
-        t = (2 * g) // GROUP * GROUP
-        total = hidden[g * GROUP:(g + 1) * GROUP, :].astype(jnp.float32)
-        gathered = jnp.zeros_like(total)
-        for d in range(N_SP):
-            x = sums[d, t:t + GROUP, :]
-            shift = (2 * d - 2 * g) % GROUP
-            if shift:
-                x = pltpu.roll(x, shift, 0)
-            gathered = jnp.where(srow // 2 == d, x, gathered)
-        h_out[g * GROUP:(g + 1) * GROUP, :] = (total + gathered).astype(jnp.bfloat16)
+    for c in range(COLS):
+        core_copy(c).wait()
+        fwd_copy(c).wait()
+        lanes = slice(c * width, (c + 1) * width)
+        for g in range(n_groups):
+            t = (2 * g) // GROUP * GROUP
+            gathered = None
+            for d in range(N_SP):
+                x = sums[c, d, t:t + GROUP, :]
+                shift = (2 * d - 2 * g) % GROUP
+                if shift:
+                    x = pltpu.roll(x, shift, 0)
+                gathered = x if gathered is None else jnp.where(srow // 2 == d, x, gathered)
+            r = slice(g * GROUP, (g + 1) * GROUP)
+            h_out[r, lanes] = (hidden[r, lanes].astype(jnp.float32) + gathered).astype(jnp.bfloat16)
 
 
 def write_kernel(dims, pos, h_in, k_vm, v_vm, new_k, new_v, k_in, v_in, h_out, k_out, v_out, k_same, v_same,
@@ -352,16 +391,16 @@
                 pltpu.VMEM((n_seq * n_heads, head), f32),
                 pltpu.VMEM((n_seq * n_heads, head), f32),
                 pltpu.VMEM((pair_rows, rows), jnp.int32),
-                pltpu.VMEM((n_groups, N_SP, pair_rows, 2 * head), f32),
-                pltpu.VMEM((n_groups, N_SP - 1, pair_rows, 2 * head), f32),
+                pltpu.VMEM((N_SP, pair_rows, rows), f32),
+                pltpu.VMEM((n_groups, N_SP, pair_rows + 8, head), f32),
+                pltpu.VMEM((n_groups, N_SP - 1, pair_rows + 8, head), f32),
                 pltpu.VMEM((own * n_heads, head), f32),
-                pltpu.VMEM((own, d_model), f32),
-                pltpu.VMEM((own, d_model), f32),
-                pltpu.VMEM((N_SP, own, d_model), f32),
+                pltpu.VMEM((COLS, own, d_model // COLS), f32),
+                pltpu.VMEM((COLS, own, d_model // COLS), f32),
+                pltpu.VMEM((COLS, N_SP, own, d_model // COLS), f32),
                 dma((W_CHUNKS,)), dma, dma((n_groups,)), dma((n_groups,)),
                 dma((n_groups, N_SP - 1)), dma((n_groups, N_SP - 1)),
-                dma, dma, dma((N_SP - 1,)), dma((N_SP - 1,)),
-            ],
+            ] + [dma((COLS,))] * 8,
             compiler_params=pltpu.CompilerParams(
                 collective_id=0, has_side_effects=True, vmem_limit_bytes=33 * MIB),
             name='attend',

time: 58.6 us -> 48.8 us (0.83)
  Pallas kernels: 57.7 us -> 47.9 us
    pallas_call x1, Pallas kernels: 45 us -> 35.2 us  [local_step(): pl.pallas_call(lambda *refs: attend_kernel(dims, *refs), out_shape=(pltpu...]
where the time goes in v3:
time: 48.8 us; the launch traced here: 48.6 us
  Pallas kernels  47.9 us (98%)
  between operations  0.66 us (1%)
    pallas_call x1, Pallas kernels, local_step(): pl.pallas_call(lambda *refs: attend_kernel(dims, *refs), out_shape=(pltpu...  35.2 us
    pallas_call x1, Pallas kernels, local_step(): pl.pallas_call(lambda *refs: write_kernel(dims, *refs), out_shape=(jax.Sh...  12.8 us

profile of v3, /device:TPU:0, one launch (start us, length us, event | category | flops | bytes accessed | tf_op | source)
XLA Modules:
  0.0 48.6 jit_solution(18323222316269525596)
XLA Ops:
  0.6 0.0 copy-start
  0.6 35.2 %attend.1 = (bf16[64,3072]{1,0:T(8,128)(2,1)S(1)}, bf16[56,1024,128]{2,1,0:T(8,128)(2,1)S(1)}, bf16[56,1024,128]{2,1,0:T(8,128)(2,1)S(1)}, f32[1024,128]{1,0:T(8,128)S(1)}, f32[1024,128]{1,0:T(8,128)S(1)}) custom-call(s32[64]{0:T(128)} %refs_0_.3, bf16[64,3072]{1,0:T(8,128)(2,1)} %refs_1_.1, bf16[24,128]{1,0:T(8,128)(2,1)} %bitcast.9, ...), custom_call_target="tpu_custom_call" | custom-call | tf_op jit(solution)/shard_map/attend/pallas_call | solution.py:372
  35.8 0.0 copy-done
  35.8 12.8 %write.1 = (bf16[64,3072]{1,0:T(8,128)(2,1)}, bf16[64,1024,128]{2,1,0:T(8,128)(2,1)}, bf16[64,1024,128]{2,1,0:T(8,128)(2,1)}, bf16[56,1024,128]{2,1,0:T(8,128)(2,1)S(1)}, bf16[56,1024,128]{2,1,0:T(8,128)(2,1)S(1)}) custom-call(s32[64]{0:T(128)S(1)} %copy-done, ...), custom_call_target="tpu_custom_call", output_to_operand_aliasing={{3}: (2, {}), {4}: (3, {})} | custom-call | tf_op jit(solution)/shard_map/write/pallas_call | solution.py:408
Async XLA Ops:
  0.6 35.2 %copy-start = (s32[64]{0:T(128)S(1)}, s32[64]{0:T(128)}, u32[]{:S(2)}) copy-start(s32[64]{0:T(128)} %refs_0_.3) | copy-start | bytes 772

commit v4 on v3

--- a/solution.py
+++ b/solution.py
@@ -11,12 +11,11 @@
 NEG = -1e30
 MIB = 1024 * 1024
 N_SP = 4
-COLS = 4
-WO_AT = 7
+COLS = 6
+WO_AT = 6
 GROUP = 8
 W_CHUNKS = 6
-W_SLOTS = 3
-AHEAD = 3
+AHEAD = 4
 HELD = 7
 JOB = 2
 SLOTS = 4
@@ -24,10 +23,10 @@
 W_VMEM = 3
 
 
-def attend_kernel(dims, pos, hidden, norm_scale, inv_freq, w_qkv, w_out, k_in, v_in,
+def attend_kernel(dims, pos_in, hidden_in, scale_in, freq_in, w_qkv, w_out, k_in, v_in,
                   h_out, k_vm, v_vm, new_k, new_v,
-                  u, wq, acc, rope_c, rope_s, wo, k_rest, v_rest, q_rows, kn_rows, vn_rows, tok, score, part, recv, merged, proj, proj_in, sums,
-                  w_sem, wo_sem, k_sem, v_sem, part_send, part_recv, tp_send, tp_recv, x_send, x_recv,
+                  pos, hidden, norm_scale, inv_freq, u, wq, acc, rope_c, rope_s, wo, k_rest, v_rest, q_rows, kn_rows, vn_rows, tok, score, part, recv, merged, proj, proj_in, sums,
+                  in_sem, w_sem, wo_sem, k_sem, v_sem, acc_send, acc_recv, part_send, part_recv, tp_send, tp_recv, x_send, x_recv,
                   core_send, core_recv, fwd_send, fwd_recv):
     n_seq, rows, kv, head, per_kv, d_model = dims
     n_heads = kv * per_kv
@@ -40,8 +39,14 @@
     seq_local = rows // kv
     scale2 = head ** -0.5 * math.log2(math.e)
 
+    core = lax.rem(sp, 2)
+    partner = sp + 1 - 2 * core
+    across = lax.rem(sp + 2, N_SP)
+    half_cols = w_qkv.shape[1] // 2
+
     def w_copy(c):
-        return pltpu.make_async_copy(w_qkv.at[pl.ds(c * w_rows, w_rows)], wq.at[c % W_SLOTS], w_sem.at[c])
+        cols = pl.ds(pl.multiple_of(core * half_cols, head), half_cols)
+        return pltpu.make_async_copy(w_qkv.at[pl.ds(c * w_rows, w_rows), cols], wq.at[c], w_sem.at[c])
 
     def held(ref, rest, n_held, g):
         return (ref, g) if g < n_held else (rest, g - n_held)
@@ -56,12 +61,12 @@
     def v_copy(g):
         return cache_copy(v_in, v_vm, v_rest, HELD, v_sem, g)
 
-    def fetch(g):
-        k_copy(g).start()
-        v_copy(g).start()
-
     wo_copy = pltpu.make_async_copy(w_out, wo, wo_sem)
-    for c in range(W_SLOTS):
+    small = [pltpu.make_async_copy(a, b, in_sem.at[i]) for i, (a, b) in enumerate(
+        ((hidden_in, hidden), (scale_in, norm_scale), (freq_in, inv_freq), (pos_in, pos)))]
+    for c in small:
+        c.start()
+    for c in range(W_CHUNKS):
         w_copy(c).start()
 
     barrier = pltpu.get_barrier_semaphore()
@@ -69,6 +74,8 @@
         pl.semaphore_signal(barrier, inc=1, device_id={'sp': lax.rem(sp + s, N_SP)}, device_id_type=MESH)
     pl.semaphore_signal(barrier, inc=1, device_id={'tp': 1 - tp}, device_id_type=MESH)
 
+    for c in small:
+        c.wait()
     hid = hidden[...].astype(jnp.float32)
     mean = jnp.mean(hid, axis=-1, keepdims=True)
     cen = hid - mean
@@ -84,7 +91,7 @@
     row_kv = lax.rem(row, n_heads) // per_kv
     tok[...] = jnp.where(lax.rem(col, kv) == row_kv, sp * seq_local + col // kv, 1 << 30)
 
-    acc[...] = jnp.zeros_like(acc)
+    acc[core] = jnp.zeros(acc.shape[1:], jnp.float32)
 
     brow = lax.broadcasted_iota(jnp.int32, (n_seq, 1), 0)
     pos_col = jnp.zeros((n_seq, 1), jnp.int32)
@@ -97,20 +104,25 @@
     rope_c[...] = c2
     rope_s[...] = s2
 
+    cache_order = [f(g) for g in range(AHEAD) for f in (k_copy, v_copy)]
     for c in range(W_CHUNKS):
         w_copy(c).wait()
-        acc[...] += jnp.dot(u[c], wq[c % W_SLOTS], preferred_element_type=jnp.float32)
-        if c + W_SLOTS < W_CHUNKS:
-            w_copy(c + W_SLOTS).start()
-        else:
-            fetch(c + W_SLOTS - W_CHUNKS)
+        for copy in cache_order[c * len(cache_order) // W_CHUNKS:(c + 1) * len(cache_order) // W_CHUNKS]:
+            copy.start()
+        acc[core] += jnp.dot(u[c], wq[c], preferred_element_type=jnp.float32)
+
+    pl.semaphore_wait(barrier, N_SP)
+    acc_copy = pltpu.make_async_remote_copy(acc.at[core], acc.at[core], acc_send, acc_recv,
+                                            device_id={'sp': partner}, device_id_type=MESH)
+    acc_copy.start()
+    acc_copy.wait()
 
     c2 = rope_c[...]
     s2 = rope_s[...]
     for g in range(kv):
         for j in range(per_kv + 2):
-            lo = (g * (per_kv + 2) + j) * head
-            x = jnp.clip(acc[:, lo:lo + head].astype(jnp.bfloat16).astype(jnp.float32), -8.0, 8.0)
+            lo = (g % (kv // 2) * (per_kv + 2) + j) * head
+            x = jnp.clip(acc[g // (kv // 2), :, lo:lo + head].astype(jnp.bfloat16).astype(jnp.float32), -8.0, 8.0)
             if j <= per_kv:
                 x = (x * c2 + pltpu.roll(x, head // 2, 1) * s2).astype(jnp.bfloat16).astype(jnp.float32)
             if j < per_kv:
@@ -121,8 +133,6 @@
                     wide[pl.ds(g * per_kv + i, n_seq, stride=n_heads), :] = x
                 for i in range(16 // kv):
                     rep[pl.ds(i * kv + g, n_seq, stride=16), :] = x
-
-    pl.semaphore_wait(barrier, N_SP)
 
     prow = lax.broadcasted_iota(jnp.int32, (pair_rows, 1), 0)
     first = prow < n_heads
@@ -222,8 +232,6 @@
         [merged[pl.ds(n, own, stride=n_heads), :].astype(jnp.bfloat16) for n in range(n_heads)], axis=1)
     wo_copy.wait()
     width = d_model // COLS
-    partner = sp + 1 - 2 * lax.rem(sp, 2)
-    across = lax.rem(sp + 2, N_SP)
 
     def tp_copy(c):
         return pltpu.make_async_remote_copy(proj.at[c], proj_in.at[c], tp_send.at[c], tp_recv.at[c],
@@ -271,8 +279,8 @@
             h_out[r, lanes] = (hidden[r, lanes].astype(jnp.float32) + gathered).astype(jnp.bfloat16)
 
 
-def write_kernel(dims, pos, h_in, k_vm, v_vm, new_k, new_v, k_in, v_in, h_out, k_out, v_out, k_same, v_same,
-                 slots, h_sem, rd_sem, wr_sem, blk_sem):
+def write_kernel(dims, pos_in, h_in, k_vm, v_vm, new_k, new_v, k_in, v_in, h_out, k_out, v_out, k_same, v_same,
+                 pos, slots, pos_sem, h_sem, rd_sem, wr_sem, blk_sem):
     n_seq, rows, kv, _, _, _ = dims
     sp = lax.axis_index('sp')
     seq_local = rows // kv
@@ -321,10 +329,13 @@
         block(n).start()
 
     n_blocks = 2 * HELD
+    pos_copy = pltpu.make_async_copy(pos_in, pos, pos_sem)
+    pos_copy.start()
     h_copy = pltpu.make_async_copy(h_in, h_out, h_sem)
     h_copy.start()
     for j in range(SLOTS):
         read(j).start()
+    pos_copy.wait()
     for n in range(n_blocks):
         if n >= WINDOW:
             block(n - WINDOW).wait()
@@ -362,7 +373,6 @@
         f32, bf16 = jnp.float32, jnp.bfloat16
         vmem = pl.BlockSpec(memory_space=pltpu.VMEM)
         hbm = pl.BlockSpec(memory_space=pltpu.HBM)
-        smem = pl.BlockSpec(memory_space=pltpu.SMEM)
         cache = (n_seq, rows, head)
         dma = pltpu.SemaphoreType.DMA
         keep = pltpu.with_memory_space_constraint
@@ -376,12 +386,16 @@
                        pltpu.VMEM((HELD * GROUP, rows, head), bf16),
                        pltpu.VMEM((n_seq * 16, head), f32),
                        pltpu.VMEM((n_seq * 16, head), f32)),
-            in_specs=[smem, vmem, vmem, vmem, hbm, hbm, hbm, hbm],
+            in_specs=[hbm] * 8,
             out_specs=(vmem,) * 5,
             scratch_shapes=[
+                pltpu.SMEM((n_seq,), jnp.int32),
+                pltpu.VMEM(hidden.shape, bf16),
+                pltpu.VMEM((d_model // head, head), bf16),
+                pltpu.VMEM((1, head), f32),
                 pltpu.VMEM((W_CHUNKS, n_seq, d_model // W_CHUNKS), bf16),
-                pltpu.VMEM((W_SLOTS, d_model // W_CHUNKS, w_qkv.shape[1]), bf16),
-                pltpu.VMEM((n_seq, w_qkv.shape[1]), f32),
+                pltpu.VMEM((W_CHUNKS, d_model // W_CHUNKS, w_qkv.shape[1] // 2), bf16),
+                pltpu.VMEM((2, n_seq, w_qkv.shape[1] // 2), f32),
                 pltpu.VMEM((n_seq, head), f32),
                 pltpu.VMEM((n_seq, head), f32),
                 pltpu.VMEM(w_out.shape, bf16),
@@ -398,28 +412,30 @@
                 pltpu.VMEM((COLS, own, d_model // COLS), f32),
                 pltpu.VMEM((COLS, own, d_model // COLS), f32),
                 pltpu.VMEM((COLS, N_SP, own, d_model // COLS), f32),
-                dma((W_CHUNKS,)), dma, dma((n_groups,)), dma((n_groups,)),
+                dma((4,)), dma((W_CHUNKS,)), dma, dma((n_groups,)), dma((n_groups,)), dma, dma,
                 dma((n_groups, N_SP - 1)), dma((n_groups, N_SP - 1)),
             ] + [dma((COLS,))] * 8,
             compiler_params=pltpu.CompilerParams(
                 collective_id=0, has_side_effects=True, vmem_limit_bytes=33 * MIB),
             name='attend',
-        )(positions, hidden, norm_scale.reshape(d_model // 128, 128), inv_freq, w_qkv, w_out, k_flat, v_flat)
+        )(keep(positions, pltpu.HBM), keep(hidden, pltpu.HBM),
+          keep(norm_scale.reshape(d_model // head, head), pltpu.HBM), inv_freq, w_qkv, w_out, k_flat, v_flat)
         h_out, k_out, v_out, _, _ = pl.pallas_call(
             lambda *refs: write_kernel(dims, *refs),
             out_shape=(jax.ShapeDtypeStruct(hidden.shape, bf16),
                        jax.ShapeDtypeStruct(cache, bf16), jax.ShapeDtypeStruct(cache, bf16),
                        pltpu.VMEM(k_vm.shape, bf16), pltpu.VMEM(v_vm.shape, bf16)),
-            in_specs=[smem] + [vmem] * 5 + [hbm] * 2,
+            in_specs=[hbm] + [vmem] * 5 + [hbm] * 2,
             out_specs=(hbm,) * 3 + (vmem,) * 2,
             input_output_aliases={2: 3, 3: 4},
             scratch_shapes=[
+                pltpu.SMEM((n_seq,), jnp.int32),
                 pltpu.VMEM((SLOTS, JOB, rows, head), bf16),
-                dma, dma((n_jobs,)), dma((n_jobs,)), dma((2 * HELD,)),
+                dma, dma, dma((n_jobs,)), dma((n_jobs,)), dma((2 * HELD,)),
             ],
             compiler_params=pltpu.CompilerParams(vmem_limit_bytes=W_VMEM * MIB),
             name='write',
-        )(positions, *[keep(x, pltpu.VMEM) for x in (h_vm, k_vm, v_vm, new_k, new_v)], k_flat, v_flat)
+        )(keep(positions, pltpu.HBM), *[keep(x, pltpu.VMEM) for x in (h_vm, k_vm, v_vm, new_k, new_v)], k_flat, v_flat)
         return h_out, k_out.reshape(k_cache.shape), v_out.reshape(v_cache.shape)
 
     return jax.shard_map(

time: 48.8 us -> 46.3 us (0.949)
  Pallas kernels: 47.9 us -> 45.4 us
    pallas_call x1, Pallas kernels: 35.2 us -> 33.3 us  [local_step(): pl.pallas_call(lambda *refs: attend_kernel(dims, *refs), out_shape=(pltpu...]
    pallas_call x1, Pallas kernels: 12.8 us -> 12.2 us  [local_step(): pl.pallas_call(lambda *refs: write_kernel(dims, *refs), out_shape=(jax.Sh...]
where the time goes in v4:
time: 46.3 us; the launch traced here: 46.1 us
  Pallas kernels  45.4 us (98%)
  between operations  0.64 us (1%)
    pallas_call x1, Pallas kernels, local_step(): pl.pallas_call(lambda *refs: attend_kernel(dims, *refs), out_shape=(pltpu...  33.3 us
    pallas_call x1, Pallas kernels, local_step(): pl.pallas_call(lambda *refs: write_kernel(dims, *refs), out_shape=(jax.Sh...  12.2 us

profile of v4, /device:TPU:0, one launch (start us, length us, event | category | flops | bytes accessed | tf_op | source)
XLA Modules:
  0.0 46.1 jit_solution(6974352121406454198)
XLA Ops:
  0.6 33.3 %attend.1 = (bf16[64,3072]{1,0:T(8,128)(2,1)S(1)}, bf16[56,1024,128]{2,1,0:T(8,128)(2,1)S(1)}, bf16[56,1024,128]{2,1,0:T(8,128)(2,1)S(1)}, f32[1024,128]{1,0:T(8,128)S(1)}, f32[1024,128]{1,0:T(8,128)S(1)}) custom-call(s32[64]{0:T(128)} %refs_0_.3, bf16[64,3072]{1,0:T(8,128)(2,1)} %refs_1_.1, bf16[24,128]{1,0:T(8,128)(2,1)} %bitcast.9, ...), custom_call_target="tpu_custom_call" | custom-call | tf_op jit(solution)/shard_map/attend/pallas_call | solution.py:382
  33.9 12.2 %write.1 = (bf16[64,3072]{1,0:T(8,128)(2,1)}, bf16[64,1024,128]{2,1,0:T(8,128)(2,1)}, bf16[64,1024,128]{2,1,0:T(8,128)(2,1)}, bf16[56,1024,128]{2,1,0:T(8,128)(2,1)S(1)}, bf16[56,1024,128]{2,1,0:T(8,128)(2,1)S(1)}) custom-call(s32[64]{0:T(128)} %refs_0_.3, ...), custom_call_target="tpu_custom_call", output_to_operand_aliasing={{3}: (2, {}), {4}: (3, {})} | custom-call | tf_op jit(solution)/shard_map/write/pallas_call | solution.py:423

commit v5 on v4

--- a/solution.py
+++ b/solution.py
@@ -12,9 +12,9 @@
 MIB = 1024 * 1024
 N_SP = 4
 COLS = 6
-WO_AT = 6
+WO_AT = 4
+PHASE = 2
 GROUP = 8
-W_CHUNKS = 6
 AHEAD = 4
 HELD = 7
 JOB = 2
@@ -25,7 +25,7 @@
 
 def attend_kernel(dims, pos_in, hidden_in, scale_in, freq_in, w_qkv, w_out, k_in, v_in,
                   h_out, k_vm, v_vm, new_k, new_v,
-                  pos, hidden, norm_scale, inv_freq, u, wq, acc, rope_c, rope_s, wo, k_rest, v_rest, q_rows, kn_rows, vn_rows, tok, score, part, recv, merged, proj, proj_in, sums,
+                  pos, hidden, norm_scale, inv_freq, u, wq, heads, rope_c, rope_s, wo, k_rest, v_rest, q_rows, kn_rows, vn_rows, tok, score, part, recv, merged, proj, proj_in, sums,
                   in_sem, w_sem, wo_sem, k_sem, v_sem, acc_send, acc_recv, part_send, part_recv, tp_send, tp_recv, x_send, x_recv,
                   core_send, core_recv, fwd_send, fwd_recv):
     n_seq, rows, kv, head, per_kv, d_model = dims
@@ -33,7 +33,6 @@
     n_groups = n_seq // GROUP
     pair_rows = 2 * n_heads
     own = n_seq // N_SP
-    w_rows = d_model // W_CHUNKS
     sp = lax.axis_index('sp')
     tp = lax.axis_index('tp')
     seq_local = rows // kv
@@ -43,10 +42,12 @@
     partner = sp + 1 - 2 * core
     across = lax.rem(sp + 2, N_SP)
     half_cols = w_qkv.shape[1] // 2
+    w_cols = 2 * head
+    w_chunks = half_cols // w_cols
 
     def w_copy(c):
-        cols = pl.ds(pl.multiple_of(core * half_cols, head), half_cols)
-        return pltpu.make_async_copy(w_qkv.at[pl.ds(c * w_rows, w_rows), cols], wq.at[c], w_sem.at[c])
+        cols = pl.ds(pl.multiple_of(core * half_cols + c * w_cols, head), w_cols)
+        return pltpu.make_async_copy(w_qkv.at[:, cols], wq.at[c], w_sem.at[c])
 
     def held(ref, rest, n_held, g):
         return (ref, g) if g < n_held else (rest, g - n_held)
@@ -66,7 +67,7 @@
         ((hidden_in, hidden), (scale_in, norm_scale), (freq_in, inv_freq), (pos_in, pos)))]
     for c in small:
         c.start()
-    for c in range(W_CHUNKS):
+    for c in range(w_chunks):
         w_copy(c).start()
 
     barrier = pltpu.get_barrier_semaphore()
@@ -83,15 +84,12 @@
     scale_rows = norm_scale[...].astype(jnp.float32)
     scale_row = jnp.concatenate([scale_rows[i:i + 1] for i in range(scale_rows.shape[0])], axis=1)
     normed = (cen * lax.rsqrt(var + 1e-5) * scale_row).astype(jnp.bfloat16)
-    for c in range(W_CHUNKS):
-        u[c] = normed[:, c * w_rows:(c + 1) * w_rows]
+    u[...] = normed
 
     col = lax.broadcasted_iota(jnp.int32, (pair_rows, rows), 1)
     row = lax.broadcasted_iota(jnp.int32, (pair_rows, rows), 0)
     row_kv = lax.rem(row, n_heads) // per_kv
     tok[...] = jnp.where(lax.rem(col, kv) == row_kv, sp * seq_local + col // kv, 1 << 30)
-
-    acc[core] = jnp.zeros(acc.shape[1:], jnp.float32)
 
     brow = lax.broadcasted_iota(jnp.int32, (n_seq, 1), 0)
     pos_col = jnp.zeros((n_seq, 1), jnp.int32)
@@ -105,26 +103,32 @@
     rope_s[...] = s2
 
     cache_order = [f(g) for g in range(AHEAD) for f in (k_copy, v_copy)]
-    for c in range(W_CHUNKS):
+    group_heads = per_kv + 2
+
+    def heads_copy(c):
+        mine = heads.at[core, pl.ds(2 * c, 2)]
+        return pltpu.make_async_remote_copy(mine, mine, acc_send.at[c], acc_recv.at[c],
+                                            device_id={'sp': partner}, device_id_type=MESH)
+
+    for c in range(w_chunks):
         w_copy(c).wait()
-        for copy in cache_order[c * len(cache_order) // W_CHUNKS:(c + 1) * len(cache_order) // W_CHUNKS]:
+        for copy in cache_order[c * len(cache_order) // w_chunks:(c + 1) * len(cache_order) // w_chunks]:
             copy.start()
-        acc[core] += jnp.dot(u[c], wq[c], preferred_element_type=jnp.float32)
-
-    pl.semaphore_wait(barrier, N_SP)
-    acc_copy = pltpu.make_async_remote_copy(acc.at[core], acc.at[core], acc_send, acc_recv,
-                                            device_id={'sp': partner}, device_id_type=MESH)
-    acc_copy.start()
-    acc_copy.wait()
-
-    c2 = rope_c[...]
-    s2 = rope_s[...]
-    for g in range(kv):
-        for j in range(per_kv + 2):
-            lo = (g % (kv // 2) * (per_kv + 2) + j) * head
-            x = jnp.clip(acc[g // (kv // 2), :, lo:lo + head].astype(jnp.bfloat16).astype(jnp.float32), -8.0, 8.0)
-            if j <= per_kv:
-                x = (x * c2 + pltpu.roll(x, head // 2, 1) * s2).astype(jnp.bfloat16).astype(jnp.float32)
+        qkv = jnp.dot(u[...], wq[c], preferred_element_type=jnp.float32)
+        for i in range(2):
+            x = jnp.clip(qkv[:, i * head:(i + 1) * head].astype(jnp.bfloat16).astype(jnp.float32), -8.0, 8.0)
+            if (2 * c + i) % group_heads <= per_kv:
+                x = x * rope_c[...] + pltpu.roll(x, head // 2, 1) * rope_s[...]
+                x = x.astype(jnp.bfloat16).astype(jnp.float32)
+            heads[core, 2 * c + i] = x
+        if c == 0:
+            pl.semaphore_wait(barrier, N_SP)
+        heads_copy(c).start()
+
+    def spread(half):
+        for h in range(half_cols // head):
+            g, j = half * (kv // 2) + h // group_heads, h % group_heads
+            x = heads[half, h]
             if j < per_kv:
                 q_rows[pl.ds(g * per_kv + j, n_seq, stride=n_heads), :] = x
             else:
@@ -134,6 +138,18 @@
                 for i in range(16 // kv):
                     rep[pl.ds(i * kv + g, n_seq, stride=16), :] = x
 
+    for half in range(2):
+        @pl.when(core == half)
+        def _():
+            spread(half)
+
+    for c in range(w_chunks):
+        heads_copy(c).wait()
+    for half in range(2):
+        @pl.when(core != half)
+        def _():
+            spread(half)
+
     prow = lax.broadcasted_iota(jnp.int32, (pair_rows, 1), 0)
     first = prow < n_heads
 
@@ -154,14 +170,14 @@
             zero = jnp.zeros_like(q)
             q_blk = jnp.concatenate([jnp.where(first, q, zero), jnp.where(first, zero, q)], axis=1).astype(jnp.bfloat16)
             k_cat = jnp.concatenate([k_ref[kb], k_ref[kb + 1]], axis=1)
-            score[d] = lax.dot_general(q_blk, k_cat, (((1,), (1,)), ((), ())), preferred_element_type=jnp.float32)
+            score[lax.rem(g, PHASE), d] = lax.dot_general(q_blk, k_cat, (((1,), (1,)), ((), ())), preferred_element_type=jnp.float32)
 
     def values(g, v_ref, v_off):
         for d in range(N_SP):
             b = g * GROUP + 2 * d
             vb = b - v_off
             limit = jnp.where(first, pos[b], pos[b + 1])
-            s = jnp.where(tok[...] < limit, score[d], NEG)
+            s = jnp.where(tok[...] < limit, score[lax.rem(g, PHASE), d], NEG)
             m = jnp.max(s, axis=-1, keepdims=True)
             w = jnp.exp2((s - m) * scale2)
             l = jnp.sum(w, axis=-1, keepdims=True)
@@ -176,30 +192,43 @@
         for s in range(1, N_SP):
             part_copy(g, s).start()
 
-    def held_step(g, carry):
-        now, later = pl.ds(g * GROUP, GROUP), pl.ds((g + AHEAD) * GROUP, GROUP)
-        pltpu.make_async_copy(k_in.at[now], k_vm.at[now], k_sem.at[g]).wait()
-        pltpu.make_async_copy(k_in.at[later], k_vm.at[later], k_sem.at[g + AHEAD]).start()
-        scores(g, k_vm, 0)
-        pltpu.make_async_copy(v_in.at[now], v_vm.at[now], v_sem.at[g]).wait()
-        pltpu.make_async_copy(v_in.at[later], v_vm.at[later], v_sem.at[g + AHEAD]).start()
-        values(g, v_vm, 0)
+    def phase_step(n, carry):
+        for g in range(PHASE):
+            g = n * PHASE + g
+            now, later = pl.ds(g * GROUP, GROUP), pl.ds((g + AHEAD) * GROUP, GROUP)
+            pltpu.make_async_copy(k_in.at[now], k_vm.at[now], k_sem.at[g]).wait()
+            pltpu.make_async_copy(k_in.at[later], k_vm.at[later], k_sem.at[g + AHEAD]).start()
+        for g in range(PHASE):
+            scores(n * PHASE + g, k_vm, 0)
+        for g in range(PHASE):
+            g = n * PHASE + g
+            now, later = pl.ds(g * GROUP, GROUP), pl.ds((g + AHEAD) * GROUP, GROUP)
+            pltpu.make_async_copy(v_in.at[now], v_vm.at[now], v_sem.at[g]).wait()
+            pltpu.make_async_copy(v_in.at[later], v_vm.at[later], v_sem.at[g + AHEAD]).start()
+        for g in range(PHASE):
+            values(n * PHASE + g, v_vm, 0)
         return carry
 
-    lax.fori_loop(0, HELD - AHEAD, held_step, 0)
-    for g in range(HELD - AHEAD, n_groups):
-        k_ref, ki = held(k_vm, k_rest, HELD, g)
-        v_ref, vi = held(v_vm, v_rest, HELD, g)
-        k_copy(g).wait()
-        if g + AHEAD < n_groups:
-            k_copy(g + AHEAD).start()
-        scores(g, k_ref, (g - ki) * GROUP)
-        v_copy(g).wait()
-        if g + AHEAD < n_groups:
-            v_copy(g + AHEAD).start()
-        if g == WO_AT:
+    looped = (HELD - AHEAD) // PHASE
+    lax.fori_loop(0, looped, phase_step, 0)
+    for n in range(looped, n_groups // PHASE):
+        gs = range(n * PHASE, (n + 1) * PHASE)
+        for g in gs:
+            k_copy(g).wait()
+            if g + AHEAD < n_groups:
+                k_copy(g + AHEAD).start()
+        for g in gs:
+            k_ref, ki = held(k_vm, k_rest, HELD, g)
+            scores(g, k_ref, (g - ki) * GROUP)
+        for g in gs:
+            v_copy(g).wait()
+            if g + AHEAD < n_groups:
+                v_copy(g + AHEAD).start()
+        if WO_AT in gs:
             wo_copy.start()
-        values(g, v_ref, (g - vi) * GROUP)
+        for g in gs:
+            v_ref, vi = held(v_vm, v_rest, HELD, g)
+            values(g, v_ref, (g - vi) * GROUP)
 
     def merge_step(g, carry):
         for s in range(1, N_SP):
@@ -366,6 +395,7 @@
         n_groups = n_seq // GROUP
         pair_rows = 2 * n_heads
         own = n_seq // N_SP
+        w_chunks = w_qkv.shape[1] // (4 * head)
         n_jobs = 2 * (n_seq - HELD * GROUP) // JOB
         dims = (n_seq, rows, kv, head, per_kv, d_model)
         half = np.arange(head) % (head // 2)
@@ -393,9 +423,9 @@
                 pltpu.VMEM(hidden.shape, bf16),
                 pltpu.VMEM((d_model // head, head), bf16),
                 pltpu.VMEM((1, head), f32),
-                pltpu.VMEM((W_CHUNKS, n_seq, d_model // W_CHUNKS), bf16),
-                pltpu.VMEM((W_CHUNKS, d_model // W_CHUNKS, w_qkv.shape[1] // 2), bf16),
-                pltpu.VMEM((2, n_seq, w_qkv.shape[1] // 2), f32),
+                pltpu.VMEM(hidden.shape, bf16),
+                pltpu.VMEM((w_chunks, d_model, 2 * head), bf16),
+                pltpu.VMEM((2, 2 * w_chunks, n_seq, head), f32),
                 pltpu.VMEM((n_seq, head), f32),
                 pltpu.VMEM((n_seq, head), f32),
                 pltpu.VMEM(w_out.shape, bf16),
@@ -405,14 +435,15 @@
                 pltpu.VMEM((n_seq * n_heads, head), f32),
                 pltpu.VMEM((n_seq * n_heads, head), f32),
                 pltpu.VMEM((pair_rows, rows), jnp.int32),
-                pltpu.VMEM((N_SP, pair_rows, rows), f32),
+                pltpu.VMEM((PHASE, N_SP, pair_rows, rows), f32),
                 pltpu.VMEM((n_groups, N_SP, pair_rows + 8, head), f32),
                 pltpu.VMEM((n_groups, N_SP - 1, pair_rows + 8, head), f32),
                 pltpu.VMEM((own * n_heads, head), f32),
                 pltpu.VMEM((COLS, own, d_model // COLS), f32),
                 pltpu.VMEM((COLS, own, d_model // COLS), f32),
                 pltpu.VMEM((COLS, N_SP, own, d_model // COLS), f32),
-                dma((4,)), dma((W_CHUNKS,)), dma, dma((n_groups,)), dma((n_groups,)), dma, dma,
+                dma((4,)), dma((w_chunks,)), dma, dma((n_groups,)), dma((n_groups,)),
+                dma((w_chunks,)), dma((w_chunks,)),
                 dma((n_groups, N_SP - 1)), dma((n_groups, N_SP - 1)),
             ] + [dma((COLS,))] * 8,
             compiler_params=pltpu.CompilerParams(

time: 46.3 us -> 46.6 us (level)
  no operation moved by 1% of the time
where the time goes in v5:
time: 46.6 us; the launch traced here: 46.4 us
  Pallas kernels  45.8 us (98%)
  between operations  0.64 us (1%)
    pallas_call x1, Pallas kernels, local_step(): pl.pallas_call(lambda *refs: attend_kernel(dims, *refs), out_shape=(pltpu...  33.6 us
    pallas_call x1, Pallas kernels, local_step(): pl.pallas_call(lambda *refs: write_kernel(dims, *refs), out_shape=(jax.Sh...  12.2 us

profile of v5, /device:TPU:0, one launch (start us, length us, event | category | flops | bytes accessed | tf_op | source)
XLA Modules:
  0.0 46.4 jit_solution(8392085715023043995)
XLA Ops:
  0.6 33.6 %attend.1 = (bf16[64,3072]{1,0:T(8,128)(2,1)S(1)}, bf16[56,1024,128]{2,1,0:T(8,128)(2,1)S(1)}, bf16[56,1024,128]{2,1,0:T(8,128)(2,1)S(1)}, f32[1024,128]{1,0:T(8,128)S(1)}, f32[1024,128]{1,0:T(8,128)S(1)}) custom-call(s32[64]{0:T(128)} %refs_0_.3, bf16[64,3072]{1,0:T(8,128)(2,1)} %refs_1_.1, bf16[24,128]{1,0:T(8,128)(2,1)} %bitcast.9, ...), custom_call_target="tpu_custom_call" | custom-call | tf_op jit(solution)/shard_map/attend/pallas_call | solution.py:412
  34.2 12.2 %write.1 = (bf16[64,3072]{1,0:T(8,128)(2,1)}, bf16[64,1024,128]{2,1,0:T(8,128)(2,1)}, bf16[64,1024,128]{2,1,0:T(8,128)(2,1)}, bf16[56,1024,128]{2,1,0:T(8,128)(2,1)S(1)}, bf16[56,1024,128]{2,1,0:T(8,128)(2,1)S(1)}) custom-call(s32[64]{0:T(128)} %refs_0_.3, ...), custom_call_target="tpu_custom_call", output_to_operand_aliasing={{3}: (2, {}), {4}: (3, {})} | custom-call | tf_op jit(solution)/shard_map/write/pallas_call | solution.py:454

commit v6 on v5

--- a/solution.py
+++ b/solution.py
@@ -11,11 +11,11 @@
 NEG = -1e30
 MIB = 1024 * 1024
 N_SP = 4
-COLS = 6
-WO_AT = 4
-PHASE = 2
+COLS = 3
+PARTS = 2
+PHASES = (3, 3, 2)
 GROUP = 8
-AHEAD = 4
+WINDOW_IN = 8
 HELD = 7
 JOB = 2
 SLOTS = 4
@@ -62,13 +62,30 @@
     def v_copy(g):
         return cache_copy(v_in, v_vm, v_rest, HELD, v_sem, g)
 
-    wo_copy = pltpu.make_async_copy(w_out, wo, wo_sem)
+    width = d_model // COLS
+
+    def wo_copy(c):
+        return pltpu.make_async_copy(w_out.at[:, pl.ds(c * width, width)], wo.at[c], wo_sem.at[c])
+
+    queue = [w_copy(c) for c in range(w_chunks)]
+    g = 0
+    for n in PHASES:
+        queue += [k_copy(i) for i in range(g, g + n)] + [v_copy(i) for i in range(g, g + n)]
+        g += n
+    queue += [wo_copy(c) for c in range(COLS)]
+    started = 0
+
+    def start(n):
+        nonlocal started
+        for copy in queue[started:started + n]:
+            copy.start()
+        started += n
+
     small = [pltpu.make_async_copy(a, b, in_sem.at[i]) for i, (a, b) in enumerate(
         ((hidden_in, hidden), (scale_in, norm_scale), (freq_in, inv_freq), (pos_in, pos)))]
     for c in small:
         c.start()
-    for c in range(w_chunks):
-        w_copy(c).start()
+    start(3)
 
     barrier = pltpu.get_barrier_semaphore()
     for s in range(1, N_SP):
@@ -86,11 +103,6 @@
     normed = (cen * lax.rsqrt(var + 1e-5) * scale_row).astype(jnp.bfloat16)
     u[...] = normed
 
-    col = lax.broadcasted_iota(jnp.int32, (pair_rows, rows), 1)
-    row = lax.broadcasted_iota(jnp.int32, (pair_rows, rows), 0)
-    row_kv = lax.rem(row, n_heads) // per_kv
-    tok[...] = jnp.where(lax.rem(col, kv) == row_kv, sp * seq_local + col // kv, 1 << 30)
-
     brow = lax.broadcasted_iota(jnp.int32, (n_seq, 1), 0)
     pos_col = jnp.zeros((n_seq, 1), jnp.int32)
     for b in range(n_seq):
@@ -102,7 +114,6 @@
     rope_c[...] = c2
     rope_s[...] = s2
 
-    cache_order = [f(g) for g in range(AHEAD) for f in (k_copy, v_copy)]
     group_heads = per_kv + 2
 
     def heads_copy(c):
@@ -112,9 +123,10 @@
 
     for c in range(w_chunks):
         w_copy(c).wait()
-        for copy in cache_order[c * len(cache_order) // w_chunks:(c + 1) * len(cache_order) // w_chunks]:
-            copy.start()
-        qkv = jnp.dot(u[...], wq[c], preferred_element_type=jnp.float32)
+        start((1, 1, 1, 1, 4)[c])
+        k_half = d_model // 2
+        qkv = (jnp.dot(u[:, :k_half], wq[c, :k_half], preferred_element_type=jnp.float32)
+               + jnp.dot(u[:, k_half:], wq[c, k_half:], preferred_element_type=jnp.float32))
         for i in range(2):
             x = jnp.clip(qkv[:, i * head:(i + 1) * head].astype(jnp.bfloat16).astype(jnp.float32), -8.0, 8.0)
             if (2 * c + i) % group_heads <= per_kv:
@@ -125,30 +137,37 @@
             pl.semaphore_wait(barrier, N_SP)
         heads_copy(c).start()
 
-    def spread(half):
+    def spread(half, queries):
         for h in range(half_cols // head):
             g, j = half * (kv // 2) + h // group_heads, h % group_heads
+            if queries != (j < per_kv):
+                continue
             x = heads[half, h]
-            if j < per_kv:
+            if queries:
                 q_rows[pl.ds(g * per_kv + j, n_seq, stride=n_heads), :] = x
-            else:
-                wide, rep = (kn_rows, new_k) if j == per_kv else (vn_rows, new_v)
-                for i in range(per_kv):
-                    wide[pl.ds(g * per_kv + i, n_seq, stride=n_heads), :] = x
-                for i in range(16 // kv):
-                    rep[pl.ds(i * kv + g, n_seq, stride=16), :] = x
+                continue
+            wide, rep = (kn_rows, new_k) if j == per_kv else (vn_rows, new_v)
+            for i in range(per_kv):
+                wide[pl.ds(g * per_kv + i, n_seq, stride=n_heads), :] = x
+            for i in range(16 // kv):
+                rep[pl.ds(i * kv + g, n_seq, stride=16), :] = x
+
+    col = lax.broadcasted_iota(jnp.int32, (pair_rows, rows), 1)
+    row = lax.broadcasted_iota(jnp.int32, (pair_rows, rows), 0)
+    row_kv = lax.rem(row, n_heads) // per_kv
+    tok[...] = jnp.where(lax.rem(col, kv) == row_kv, sp * seq_local + col // kv, 1 << 30)
 
     for half in range(2):
         @pl.when(core == half)
         def _():
-            spread(half)
+            spread(half, True)
 
     for c in range(w_chunks):
         heads_copy(c).wait()
     for half in range(2):
         @pl.when(core != half)
         def _():
-            spread(half)
+            spread(half, True)
 
     prow = lax.broadcasted_iota(jnp.int32, (pair_rows, 1), 0)
     first = prow < n_heads
@@ -163,21 +182,21 @@
     lane = lax.broadcasted_iota(jnp.int32, (8, head), 1)
     n_stat = pair_rows // 8
 
-    def scores(g, k_ref, k_off):
+    def scores(g, buf, k_ref, k_off):
         for d in range(N_SP):
             kb = g * GROUP + 2 * d - k_off
             q = q_rows[pl.ds(pl.multiple_of((g * N_SP + d) * pair_rows, 8), pair_rows), :]
             zero = jnp.zeros_like(q)
             q_blk = jnp.concatenate([jnp.where(first, q, zero), jnp.where(first, zero, q)], axis=1).astype(jnp.bfloat16)
             k_cat = jnp.concatenate([k_ref[kb], k_ref[kb + 1]], axis=1)
-            score[lax.rem(g, PHASE), d] = lax.dot_general(q_blk, k_cat, (((1,), (1,)), ((), ())), preferred_element_type=jnp.float32)
-
-    def values(g, v_ref, v_off):
+            score[buf, d] = lax.dot_general(q_blk, k_cat, (((1,), (1,)), ((), ())), preferred_element_type=jnp.float32)
+
+    def values(g, buf, v_ref, v_off):
         for d in range(N_SP):
             b = g * GROUP + 2 * d
             vb = b - v_off
             limit = jnp.where(first, pos[b], pos[b + 1])
-            s = jnp.where(tok[...] < limit, score[lax.rem(g, PHASE), d], NEG)
+            s = jnp.where(tok[...] < limit, score[buf, d], NEG)
             m = jnp.max(s, axis=-1, keepdims=True)
             w = jnp.exp2((s - m) * scale2)
             l = jnp.sum(w, axis=-1, keepdims=True)
@@ -192,44 +211,26 @@
         for s in range(1, N_SP):
             part_copy(g, s).start()
 
-    def phase_step(n, carry):
-        for g in range(PHASE):
-            g = n * PHASE + g
-            now, later = pl.ds(g * GROUP, GROUP), pl.ds((g + AHEAD) * GROUP, GROUP)
-            pltpu.make_async_copy(k_in.at[now], k_vm.at[now], k_sem.at[g]).wait()
-            pltpu.make_async_copy(k_in.at[later], k_vm.at[later], k_sem.at[g + AHEAD]).start()
-        for g in range(PHASE):
-            scores(n * PHASE + g, k_vm, 0)
-        for g in range(PHASE):
-            g = n * PHASE + g
-            now, later = pl.ds(g * GROUP, GROUP), pl.ds((g + AHEAD) * GROUP, GROUP)
-            pltpu.make_async_copy(v_in.at[now], v_vm.at[now], v_sem.at[g]).wait()
-            pltpu.make_async_copy(v_in.at[later], v_vm.at[later], v_sem.at[g + AHEAD]).start()
-        for g in range(PHASE):
-            values(n * PHASE + g, v_vm, 0)
-        return carry
-
-    looped = (HELD - AHEAD) // PHASE
-    lax.fori_loop(0, looped, phase_step, 0)
-    for n in range(looped, n_groups // PHASE):
-        gs = range(n * PHASE, (n + 1) * PHASE)
-        for g in gs:
-            k_copy(g).wait()
-            if g + AHEAD < n_groups:
-                k_copy(g + AHEAD).start()
-        for g in gs:
-            k_ref, ki = held(k_vm, k_rest, HELD, g)
-            scores(g, k_ref, (g - ki) * GROUP)
-        for g in gs:
-            v_copy(g).wait()
-            if g + AHEAD < n_groups:
-                v_copy(g + AHEAD).start()
-        if WO_AT in gs:
-            wo_copy.start()
-        for g in gs:
-            v_ref, vi = held(v_vm, v_rest, HELD, g)
-            values(g, v_ref, (g - vi) * GROUP)
-
+    g = 0
+    for n in PHASES:
+        gs = range(g, g + n)
+        g += n
+        if g == n_groups:
+            for half in range(2):
+                spread(half, False)
+        for i in gs:
+            k_copy(i).wait()
+            start(1)
+        for i in gs:
+            k_ref, ki = held(k_vm, k_rest, HELD, i)
+            scores(i, i - gs[0], k_ref, (i - ki) * GROUP)
+        for i in gs:
+            v_copy(i).wait()
+            start(1)
+        for i in gs:
+            v_ref, vi = held(v_vm, v_rest, HELD, i)
+            values(i, i - gs[0], v_ref, (i - vi) * GROUP)
+    start(len(queue))
     def merge_step(g, carry):
         for s in range(1, N_SP):
             part_copy(g, s).wait()
@@ -256,56 +257,75 @@
         merged[pl.ds(pl.multiple_of(g * pair_rows, 8), pair_rows), :] = o / l
         return carry
 
-    lax.fori_loop(0, n_groups, merge_step, 0)
-    attn = jnp.concatenate(
-        [merged[pl.ds(n, own, stride=n_heads), :].astype(jnp.bfloat16) for n in range(n_heads)], axis=1)
-    wo_copy.wait()
-    width = d_model // COLS
-
-    def tp_copy(c):
-        return pltpu.make_async_remote_copy(proj.at[c], proj_in.at[c], tp_send.at[c], tp_recv.at[c],
+    def tp_copy(p, c):
+        return pltpu.make_async_remote_copy(proj.at[p, c], proj_in.at[p, c], tp_send.at[p, c], tp_recv.at[p, c],
                                             device_id={'tp': 1 - tp}, device_id_type=MESH)
 
-    def x_copy(c):
-        return pltpu.make_async_remote_copy(sums.at[c, sp], sums.at[c, sp], x_send.at[c], x_recv.at[c],
+    def x_copy(p, c):
+        return pltpu.make_async_remote_copy(sums.at[p, c, sp], sums.at[p, c, sp], x_send.at[p, c], x_recv.at[p, c],
                                             device_id={'sp': across}, device_id_type=MESH)
 
-    def core_copy(c):
-        return pltpu.make_async_remote_copy(sums.at[c, sp], sums.at[c, sp], core_send.at[c], core_recv.at[c],
+    def core_copy(p, c):
+        return pltpu.make_async_remote_copy(sums.at[p, c, sp], sums.at[p, c, sp], core_send.at[p, c], core_recv.at[p, c],
                                             device_id={'sp': partner}, device_id_type=MESH)
 
-    def fwd_copy(c):
-        return pltpu.make_async_remote_copy(sums.at[c, across], sums.at[c, across], fwd_send.at[c], fwd_recv.at[c],
+    def fwd_copy(p, c):
+        return pltpu.make_async_remote_copy(sums.at[p, c, across], sums.at[p, c, across], fwd_send.at[p, c], fwd_recv.at[p, c],
                                             device_id={'sp': partner}, device_id_type=MESH)
 
+    part_groups = n_groups // PARTS
+    part_rows = own // PARTS
+
+    def gather_heads(p):
+        lax.fori_loop(p * part_groups, (p + 1) * part_groups, merge_step, 0)
+        first_row = p * part_groups * pair_rows
+        return jnp.concatenate([merged[pl.ds(first_row + n, part_rows, stride=n_heads), :].astype(jnp.bfloat16)
+                                for n in range(n_heads)], axis=1)
+
+    def project(p, c, attn):
+        proj[p, c] = jnp.dot(attn, wo[c], preferred_element_type=jnp.float32)
+        tp_copy(p, c).start()
+
+    def add_tp(p, c):
+        tp_copy(p, c).wait()
+        sums[p, c, sp] = proj[p, c] + proj_in[p, c]
+        x_copy(p, c).start()
+        core_copy(p, c).start()
+
+    def forward(p, c):
+        x_copy(p, c).wait()
+        fwd_copy(p, c).start()
+
+    attn = gather_heads(0)
     for c in range(COLS):
-        proj[c] = jnp.dot(attn, wo[:, c * width:(c + 1) * width], preferred_element_type=jnp.float32)
-        tp_copy(c).start()
+        wo_copy(c).wait()
+        project(0, c, attn)
+    attn = gather_heads(1)
     for c in range(COLS):
-        tp_copy(c).wait()
-        sums[c, sp] = proj[c] + proj_in[c]
-        x_copy(c).start()
-        core_copy(c).start()
+        project(1, c, attn)
+        add_tp(0, c)
     for c in range(COLS):
-        x_copy(c).wait()
-        fwd_copy(c).start()
+        add_tp(1, c)
+        forward(0, c)
+    for c in range(COLS):
+        forward(1, c)
 
     srow = lax.broadcasted_iota(jnp.int32, (GROUP, 1), 0)
-    for c in range(COLS):
-        core_copy(c).wait()
-        fwd_copy(c).wait()
-        lanes = slice(c * width, (c + 1) * width)
-        for g in range(n_groups):
-            t = (2 * g) // GROUP * GROUP
-            gathered = None
-            for d in range(N_SP):
-                x = sums[c, d, t:t + GROUP, :]
-                shift = (2 * d - 2 * g) % GROUP
-                if shift:
-                    x = pltpu.roll(x, shift, 0)
-                gathered = x if gathered is None else jnp.where(srow // 2 == d, x, gathered)
-            r = slice(g * GROUP, (g + 1) * GROUP)
-            h_out[r, lanes] = (hidden[r, lanes].astype(jnp.float32) + gathered).astype(jnp.bfloat16)
+    for p in range(PARTS):
+        for c in range(COLS):
+            core_copy(p, c).wait()
+            fwd_copy(p, c).wait()
+            lanes = slice(c * width, (c + 1) * width)
+            for i in range(part_groups):
+                gathered = None
+                for d in range(N_SP):
+                    x = sums[p, c, d]
+                    shift = (2 * d - 2 * i) % GROUP
+                    if shift:
+                        x = pltpu.roll(x, shift, 0)
+                    gathered = x if gathered is None else jnp.where(srow // 2 == d, x, gathered)
+                r = slice((p * part_groups + i) * GROUP, (p * part_groups + i + 1) * GROUP)
+                h_out[r, lanes] = (hidden[r, lanes].astype(jnp.float32) + gathered).astype(jnp.bfloat16)
 
 
 def write_kernel(dims, pos_in, h_in, k_vm, v_vm, new_k, new_v, k_in, v_in, h_out, k_out, v_out, k_same, v_same,
@@ -428,24 +448,24 @@
                 pltpu.VMEM((2, 2 * w_chunks, n_seq, head), f32),
                 pltpu.VMEM((n_seq, head), f32),
                 pltpu.VMEM((n_seq, head), f32),
-                pltpu.VMEM(w_out.shape, bf16),
+                pltpu.VMEM((COLS, w_out.shape[0], d_model // COLS), bf16),
                 pltpu.VMEM((n_seq - HELD * GROUP, rows, head), bf16),
                 pltpu.VMEM((n_seq - HELD * GROUP, rows, head), bf16),
                 pltpu.VMEM((n_seq * n_heads, head), f32),
                 pltpu.VMEM((n_seq * n_heads, head), f32),
                 pltpu.VMEM((n_seq * n_heads, head), f32),
                 pltpu.VMEM((pair_rows, rows), jnp.int32),
-                pltpu.VMEM((PHASE, N_SP, pair_rows, rows), f32),
+                pltpu.VMEM((max(PHASES), N_SP, pair_rows, rows), f32),
                 pltpu.VMEM((n_groups, N_SP, pair_rows + 8, head), f32),
                 pltpu.VMEM((n_groups, N_SP - 1, pair_rows + 8, head), f32),
                 pltpu.VMEM((own * n_heads, head), f32),
-                pltpu.VMEM((COLS, own, d_model // COLS), f32),
-                pltpu.VMEM((COLS, own, d_model // COLS), f32),
-                pltpu.VMEM((COLS, N_SP, own, d_model // COLS), f32),
-                dma((4,)), dma((w_chunks,)), dma, dma((n_groups,)), dma((n_groups,)),
+                pltpu.VMEM((PARTS, COLS, own // PARTS, d_model // COLS), f32),
+                pltpu.VMEM((PARTS, COLS, own // PARTS, d_model // COLS), f32),
+                pltpu.VMEM((PARTS, COLS, N_SP, own // PARTS, d_model // COLS), f32),
+                dma((4,)), dma((w_chunks,)), dma((COLS,)), dma((n_groups,)), dma((n_groups,)),
                 dma((w_chunks,)), dma((w_chunks,)),
                 dma((n_groups, N_SP - 1)), dma((n_groups, N_SP - 1)),
-            ] + [dma((COLS,))] * 8,
+            ] + [dma((PARTS, COLS))] * 8,
             compiler_params=pltpu.CompilerParams(
                 collective_id=0, has_side_effects=True, vmem_limit_bytes=33 * MIB),
             name='attend',

time: 46.6 us -> 45 us (0.966)
  Pallas kernels: 45.8 us -> 44.2 us
    pallas_call x1, Pallas kernels: 33.6 us -> 32 us  [local_step(): pl.pallas_call(lambda *refs: attend_kernel(dims, *refs), out_shape=(pltpu...]
where the time goes in v6:
time: 45 us; the launch traced here: 44.8 us
  Pallas kernels  44.2 us (98%)
  between operations  0.64 us (1%)
    pallas_call x1, Pallas kernels, local_step(): pl.pallas_call(lambda *refs: attend_kernel(dims, *refs), out_shape=(pltpu...  32 us
    pallas_call x1, Pallas kernels, local_step(): pl.pallas_call(lambda *refs: write_kernel(dims, *refs), out_shape=(jax.Sh...  12.2 us

profile of v6, /device:TPU:0, one launch (start us, length us, event | category | flops | bytes accessed | tf_op | source)
XLA Modules:
  0.0 44.8 jit_solution(8736697635411614063)
XLA Ops:
  0.6 32.0 %attend.1 = (bf16[64,3072]{1,0:T(8,128)(2,1)S(1)}, bf16[56,1024,128]{2,1,0:T(8,128)(2,1)S(1)}, bf16[56,1024,128]{2,1,0:T(8,128)(2,1)S(1)}, f32[1024,128]{1,0:T(8,128)S(1)}, f32[1024,128]{1,0:T(8,128)S(1)}) custom-call(s32[64]{0:T(128)} %refs_0_.3, bf16[64,3072]{1,0:T(8,128)(2,1)} %refs_1_.1, bf16[24,128]{1,0:T(8,128)(2,1)} %bitcast.9, ...), custom_call_target="tpu_custom_call" | custom-call | tf_op jit(solution)/shard_map/attend/pallas_call | solution.py:432
  32.7 12.2 %write.1 = (bf16[64,3072]{1,0:T(8,128)(2,1)}, bf16[64,1024,128]{2,1,0:T(8,128)(2,1)}, bf16[64,1024,128]{2,1,0:T(8,128)(2,1)}, bf16[56,1024,128]{2,1,0:T(8,128)(2,1)S(1)}, bf16[56,1024,128]{2,1,0:T(8,128)(2,1)S(1)}) custom-call(s32[64]{0:T(128)} %refs_0_.3, ...), custom_call_target="tpu_custom_call", output_to_operand_aliasing={{3}: (2, {}), {4}: (3, {})} | custom-call | tf_op jit(solution)/shard_map/write/pallas_call | solution.py:474

commit v7 on v6

--- a/solution.py
+++ b/solution.py
@@ -13,9 +13,10 @@
 N_SP = 4
 COLS = 3
 PARTS = 2
-PHASES = (3, 3, 2)
+PHASES = (2, 2, 2, 2)
 GROUP = 8
-WINDOW_IN = 8
+FIRST = 3
+STARTS = (1, 1, 1, 2, 4)
 HELD = 7
 JOB = 2
 SLOTS = 4
@@ -85,7 +86,7 @@
         ((hidden_in, hidden), (scale_in, norm_scale), (freq_in, inv_freq), (pos_in, pos)))]
     for c in small:
         c.start()
-    start(3)
+    start(FIRST)
 
     barrier = pltpu.get_barrier_semaphore()
     for s in range(1, N_SP):
@@ -123,7 +124,7 @@
 
     for c in range(w_chunks):
         w_copy(c).wait()
-        start((1, 1, 1, 1, 4)[c])
+        start(STARTS[c])
         k_half = d_model // 2
         qkv = (jnp.dot(u[:, :k_half], wq[c, :k_half], preferred_element_type=jnp.float32)
                + jnp.dot(u[:, k_half:], wq[c, k_half:], preferred_element_type=jnp.float32))
@@ -162,7 +163,7 @@
         def _():
             spread(half, True)
 
-    for c in range(w_chunks):
+    for c in range(w_chunks - 1):
         heads_copy(c).wait()
     for half in range(2):
         @pl.when(core != half)
@@ -216,6 +217,7 @@
         gs = range(g, g + n)
         g += n
         if g == n_groups:
+            heads_copy(w_chunks - 1).wait()
             for half in range(2):
                 spread(half, False)
         for i in gs:

time: 45 us -> 44.5 us (0.989)
  Pallas kernels: 44.2 us -> 43.6 us
    pallas_call x1, Pallas kernels: 32 us -> 31.5 us  [local_step(): pl.pallas_call(lambda *refs: attend_kernel(dims, *refs), out_shape=(pltpu...]
where the time goes in v7:
time: 44.5 us; the launch traced here: 44.3 us
  Pallas kernels  43.6 us (98%)
  between operations  0.64 us (1%)
    pallas_call x1, Pallas kernels, local_step(): pl.pallas_call(lambda *refs: attend_kernel(dims, *refs), out_shape=(pltpu...  31.5 us
    pallas_call x1, Pallas kernels, local_step(): pl.pallas_call(lambda *refs: write_kernel(dims, *refs), out_shape=(jax.Sh...  12.2 us

profile of v7, /device:TPU:0, one launch (start us, length us, event | category | flops | bytes accessed | tf_op | source)
XLA Modules:
  0.0 44.3 jit_solution(5915019209500990821)
XLA Ops:
  0.6 31.5 %attend.1 = (bf16[64,3072]{1,0:T(8,128)(2,1)S(1)}, bf16[56,1024,128]{2,1,0:T(8,128)(2,1)S(1)}, bf16[56,1024,128]{2,1,0:T(8,128)(2,1)S(1)}, f32[1024,128]{1,0:T(8,128)S(1)}, f32[1024,128]{1,0:T(8,128)S(1)}) custom-call(s32[64]{0:T(128)} %refs_0_.3, bf16[64,3072]{1,0:T(8,128)(2,1)} %refs_1_.1, bf16[24,128]{1,0:T(8,128)(2,1)} %bitcast.9, ...), custom_call_target="tpu_custom_call" | custom-call | tf_op jit(solution)/shard_map/attend/pallas_call | solution.py:434
  32.1 12.2 %write.1 = (bf16[64,3072]{1,0:T(8,128)(2,1)}, bf16[64,1024,128]{2,1,0:T(8,128)(2,1)}, bf16[64,1024,128]{2,1,0:T(8,128)(2,1)}, bf16[56,1024,128]{2,1,0:T(8,128)(2,1)S(1)}, bf16[56,1024,128]{2,1,0:T(8,128)(2,1)S(1)}) custom-call(s32[64]{0:T(128)} %refs_0_.3, ...), custom_call_target="tpu_custom_call", output_to_operand_aliasing={{3}: (2, {}), {4}: (3, {})} | custom-call | tf_op jit(solution)/shard_map/write/pallas_call | solution.py:476

commit v8 on v7

--- a/solution.py
+++ b/solution.py
@@ -13,6 +13,7 @@
 N_SP = 4
 COLS = 3
 PARTS = 2
+MERGES = (((0, 1, 2, 3),), ((4, 5), (6, 7)))
 PHASES = (2, 2, 2, 2)
 GROUP = 8
 FIRST = 3
@@ -198,7 +199,7 @@
             vb = b - v_off
             limit = jnp.where(first, pos[b], pos[b + 1])
             s = jnp.where(tok[...] < limit, score[buf, d], NEG)
-            m = jnp.max(s, axis=-1, keepdims=True)
+            m = jnp.maximum(jnp.max(s, axis=-1, keepdims=True), NEG / 2)
             w = jnp.exp2((s - m) * scale2)
             l = jnp.sum(w, axis=-1, keepdims=True)
             v_cat = jnp.concatenate([v_ref[vb], v_ref[vb + 1]], axis=1)
@@ -233,9 +234,7 @@
             v_ref, vi = held(v_vm, v_rest, HELD, i)
             values(i, i - gs[0], v_ref, (i - vi) * GROUP)
     start(len(queue))
-    def merge_step(g, carry):
-        for s in range(1, N_SP):
-            part_copy(g, s).wait()
+    def merge(g):
         r = pl.ds(pl.multiple_of((g * N_SP + sp) * pair_rows, 8), pair_rows)
         s_new = jnp.sum(q_rows[r, :] * kn_rows[r, :], axis=-1, keepdims=True)
         outs = [part[g, sp]] + [recv[g, s] for s in range(N_SP - 1)]
@@ -257,7 +256,6 @@
             o = o + f * x[:pair_rows]
             l = l + f * ll
         merged[pl.ds(pl.multiple_of(g * pair_rows, 8), pair_rows), :] = o / l
-        return carry
 
     def tp_copy(p, c):
         return pltpu.make_async_remote_copy(proj.at[p, c], proj_in.at[p, c], tp_send.at[p, c], tp_recv.at[p, c],
@@ -279,7 +277,12 @@
     part_rows = own // PARTS
 
     def gather_heads(p):
-        lax.fori_loop(p * part_groups, (p + 1) * part_groups, merge_step, 0)
+        for gs in MERGES[p]:
+            for g in gs:
+                for s in range(1, N_SP):
+                    part_copy(g, s).wait()
+            for g in gs:
+                merge(g)
         first_row = p * part_groups * pair_rows
         return jnp.concatenate([merged[pl.ds(first_row + n, part_rows, stride=n_heads), :].astype(jnp.bfloat16)
                                 for n in range(n_heads)], axis=1)

time: 44.5 us -> 44.1 us (level)
  no operation moved by 1% of the time
where the time goes in v8:
time: 44.1 us; the launch traced here: 43.9 us
  Pallas kernels  43.2 us (98%)
  between operations  0.64 us (1%)
    pallas_call x1, Pallas kernels, local_step(): pl.pallas_call(lambda *refs: attend_kernel(dims, *refs), out_shape=(pltpu...  31.1 us
    pallas_call x1, Pallas kernels, local_step(): pl.pallas_call(lambda *refs: write_kernel(dims, *refs), out_shape=(jax.Sh...  12.2 us

profile of v8, /device:TPU:0, one launch (start us, length us, event | category | flops | bytes accessed | tf_op | source)
XLA Modules:
  0.0 43.9 jit_solution(14735228340636170411)
XLA Ops:
  0.6 31.1 %attend.1 = (bf16[64,3072]{1,0:T(8,128)(2,1)S(1)}, bf16[56,1024,128]{2,1,0:T(8,128)(2,1)S(1)}, bf16[56,1024,128]{2,1,0:T(8,128)(2,1)S(1)}, f32[1024,128]{1,0:T(8,128)S(1)}, f32[1024,128]{1,0:T(8,128)S(1)}) custom-call(s32[64]{0:T(128)} %refs_0_.3, bf16[64,3072]{1,0:T(8,128)(2,1)} %refs_1_.1, bf16[24,128]{1,0:T(8,128)(2,1)} %bitcast.9, ...), custom_call_target="tpu_custom_call" | custom-call | tf_op jit(solution)/shard_map/attend/pallas_call | solution.py:437
  31.7 12.2 %write.1 = (bf16[64,3072]{1,0:T(8,128)(2,1)}, bf16[64,1024,128]{2,1,0:T(8,128)(2,1)}, bf16[64,1024,128]{2,1,0:T(8,128)(2,1)}, bf16[56,1024,128]{2,1,0:T(8,128)(2,1)S(1)}, bf16[56,1024,128]{2,1,0:T(8,128)(2,1)S(1)}) custom-call(s32[64]{0:T(128)} %refs_0_.3, ...), custom_call_target="tpu_custom_call", output_to_operand_aliasing={{3}: (2, {}), {4}: (3, {})} | custom-call | tf_op jit(solution)/shard_map/write/pallas_call | solution.py:479

commit v9 on v8

--- a/solution.py
+++ b/solution.py
@@ -148,11 +148,16 @@
             if queries:
                 q_rows[pl.ds(g * per_kv + j, n_seq, stride=n_heads), :] = x
                 continue
-            wide, rep = (kn_rows, new_k) if j == per_kv else (vn_rows, new_v)
+            wide = kn_rows if j == per_kv else vn_rows
             for i in range(per_kv):
                 wide[pl.ds(g * per_kv + i, n_seq, stride=n_heads), :] = x
-            for i in range(16 // kv):
-                rep[pl.ds(i * kv + g, n_seq, stride=16), :] = x
+
+    def repeat_rows():
+        for g in range(kv):
+            for j, rep in ((per_kv, new_k), (per_kv + 1, new_v)):
+                x = heads[g // (kv // 2), g % (kv // 2) * group_heads + j]
+                for i in range(16 // kv):
+                    rep[pl.ds(i * kv + g, n_seq, stride=16), :] = x
 
     col = lax.broadcasted_iota(jnp.int32, (pair_rows, rows), 1)
     row = lax.broadcasted_iota(jnp.int32, (pair_rows, rows), 0)
@@ -309,6 +314,7 @@
     for c in range(COLS):
         project(1, c, attn)
         add_tp(0, c)
+    repeat_rows()
     for c in range(COLS):
         add_tp(1, c)
         forward(0, c)

time: 44.1 us -> 43.8 us (level)
  no operation moved by 1% of the time
where the time goes in v9:
time: 43.8 us; the launch traced here: 43.6 us
  Pallas kernels  43 us (98%)
  between operations  0.64 us (1%)
    pallas_call x1, Pallas kernels, local_step(): pl.pallas_call(lambda *refs: attend_kernel(dims, *refs), out_shape=(pltpu...  30.8 us
    pallas_call x1, Pallas kernels, local_step(): pl.pallas_call(lambda *refs: write_kernel(dims, *refs), out_shape=(jax.Sh...  12.2 us

profile of v9, /device:TPU:0, one launch (start us, length us, event | category | flops | bytes accessed | tf_op | source)
XLA Modules:
  0.0 43.6 jit_solution(1490089369213091568)
XLA Ops:
  0.6 30.8 %attend.1 = (bf16[64,3072]{1,0:T(8,128)(2,1)S(1)}, bf16[56,1024,128]{2,1,0:T(8,128)(2,1)S(1)}, bf16[56,1024,128]{2,1,0:T(8,128)(2,1)S(1)}, f32[1024,128]{1,0:T(8,128)S(1)}, f32[1024,128]{1,0:T(8,128)S(1)}) custom-call(s32[64]{0:T(128)} %refs_0_.3, bf16[64,3072]{1,0:T(8,128)(2,1)} %refs_1_.1, bf16[24,128]{1,0:T(8,128)(2,1)} %bitcast.9, ...), custom_call_target="tpu_custom_call" | custom-call | tf_op jit(solution)/shard_map/attend/pallas_call | solution.py:443
  31.4 12.2 %write.1 = (bf16[64,3072]{1,0:T(8,128)(2,1)}, bf16[64,1024,128]{2,1,0:T(8,128)(2,1)}, bf16[64,1024,128]{2,1,0:T(8,128)(2,1)}, bf16[56,1024,128]{2,1,0:T(8,128)(2,1)S(1)}, bf16[56,1024,128]{2,1,0:T(8,128)(2,1)S(1)}) custom-call(s32[64]{0:T(128)} %refs_0_.3, ...), custom_call_target="tpu_custom_call", output_to_operand_aliasing={{3}: (2, {}), {4}: (3, {})} | custom-call | tf_op jit(solution)/shard_map/write/pallas_call | solution.py:485
